TPU v7x, 256 devices: a whole 4x4x8 slice. The times are simulated.
256 devices in a mesh: item: 16 (over x, y), user: 8 (over z), edge: 2 (over core).
Axes of the slice: x: 4, y: 4, z: 8, core: 2. Of those that a mesh axis runs over, the one named last changes fastest.
Arguments:
- item_emb: bfloat16 [65536, 256], P('item'), may hold values from -6 to 6
- user_emb: bfloat16 [49152, 256], P('user'), may hold values from -6 to 6
- block_item: int32 [16, 8, 2, 96], P('item', 'user', 'edge'), may hold values from 0 to 31
- block_user: int32 [16, 8, 2, 96], P('item', 'user', 'edge'), may hold values from 0 to 47
- block_rows: int32 [16, 8, 2, 96, 128], P('item', 'user', 'edge'), may hold values from 0 to 127
- block_count: int32 [16, 8, 2], P('item', 'user', 'edge'), may hold values from 1 to 96, as said below
- user_weight: bfloat16 [256, 256], replicated, may hold values from -7 to 7
- up_weight: bfloat16 [256, 1024], replicated, may hold values from -0.375 to 0.375
- down_weight: bfloat16 [1024, 256], replicated, may hold values from -0.1875 to 0.1875
Outputs:
- new_items: bfloat16 [65536, 256], P(('item', 'user', 'edge'))
Inputs may be any that keep to these rules, and one draw needn't show every extreme that they name: `block_count`: some list has exactly 96 live slots in every draw; entries of slots that are not live are ignored.
All inputs are finite; a program needn't handle non-finite values.
Results may differ from a plain program's by a relative error of at most 0.0045.
Values may be sent and summed in bfloat16 or wider, within the bound.
A program may use at most 64 MiB of HBM per device.

v0:
```python
import jax
import jax.numpy as jnp
from jax import lax
from jax.sharding import PartitionSpec as P

TILE = 128


def refresh(summed, degree, own_rows, user_weight):
    average = (summed / jnp.maximum(degree, 1.0)[:, None]).astype(jnp.bfloat16)
    projected = jnp.dot(average, user_weight, preferred_element_type=jnp.float32)
    return (own_rows.astype(jnp.float32) + jax.nn.silu(projected)).astype(jnp.bfloat16)


def body(
    item_emb,
    user_emb,
    block_item,
    block_user,
    block_rows,
    block_count,
    user_weight,
    up_weight,
    down_weight,
):
    channels = item_emb.shape[1]
    item_tiles = item_emb.shape[0] // TILE
    user_tiles = user_emb.shape[0] // TILE
    slot_items = block_item.reshape(-1)
    slot_users = block_user.reshape(-1)
    slot_links = block_rows.reshape(-1, TILE)
    live_count = block_count.reshape(())
    slots = slot_items.shape[0]
    per_turn = min(32, slots)
    rounds = (live_count + per_turn - 1) // per_turn
    inside = jnp.arange(TILE, dtype=jnp.int32)
    tiled_items = item_emb.reshape(item_tiles, TILE, channels)

    def pieces(which):
        offset = which * per_turn
        items_at = lax.dynamic_slice_in_dim(slot_items, offset, per_turn, 0)
        users_at = lax.dynamic_slice_in_dim(slot_users, offset, per_turn, 0)
        links = lax.dynamic_slice_in_dim(slot_links, offset, per_turn, 0)
        alive = offset + jnp.arange(per_turn, dtype=jnp.int32) < live_count
        onehot = ((links[:, :, None] == inside[None, None, :]) & alive[:, None, None]).astype(
            jnp.bfloat16
        )
        return (items_at, users_at, onehot, alive)

    def first_hop(which, carry):
        summed, degree = carry
        items_at, users_at, onehot, alive = pieces(which)
        gathered = jnp.take(tiled_items, items_at, axis=0)
        contrib = jnp.einsum("grc,grd->gcd", onehot, gathered, preferred_element_type=jnp.float32)
        chooser = (jnp.arange(user_tiles, dtype=jnp.int32)[:, None] == users_at[None, :]).astype(
            jnp.float32
        )
        summed = summed + jnp.einsum(
            "sg,gcd->scd", chooser, contrib, precision=lax.Precision.HIGHEST
        )
        column_hits = jnp.sum(onehot.astype(jnp.float32), axis=1)
        degree = degree + jnp.dot(chooser, column_hits, precision=lax.Precision.HIGHEST)
        return (summed, degree)

    start = (
        jnp.zeros((user_tiles, TILE, channels), jnp.float32),
        jnp.zeros((user_tiles, TILE), jnp.float32),
    )
    user_part, user_hits = lax.fori_loop(0, rounds, first_hop, start)
    user_part = user_part.reshape(-1, channels)
    user_hits = user_hits.reshape(-1)
    whole_sum, whole_hits = lax.psum((user_part, user_hits), ("item", "edge"))
    user_new = refresh(whole_sum, whole_hits, user_emb, user_weight)
    tiled_users = user_new.reshape(user_tiles, TILE, channels)

    def second_hop(which, carry):
        summed, degree = carry
        items_at, users_at, onehot, alive = pieces(which)
        gathered = jnp.take(tiled_users, users_at, axis=0)
        contrib = jnp.einsum("grc,gcd->grd", onehot, gathered, preferred_element_type=jnp.float32)
        chooser = (
            (jnp.arange(item_tiles, dtype=jnp.int32)[:, None] == items_at[None, :]) & alive[None, :]
        ).astype(jnp.float32)
        summed = summed + jnp.einsum(
            "sg,grd->srd", chooser, contrib, precision=lax.Precision.HIGHEST
        )
        degree = degree + jnp.sum(chooser, axis=1)
        return (summed, degree)

    start = (
        jnp.zeros((item_tiles, TILE, channels), jnp.float32),
        jnp.zeros((item_tiles,), jnp.float32),
    )
    item_part, tile_hits = lax.fori_loop(0, rounds, second_hop, start)
    item_part = item_part.reshape(-1, channels)
    item_hits = jnp.broadcast_to(tile_hits[:, None], (item_tiles, TILE)).reshape(-1)
    edge_count = lax.axis_size("edge")
    item_sum, item_degree = (
        lax.psum_scatter(item_part, ("user", "edge"), scatter_dimension=0, tiled=True),
        lax.psum_scatter(item_hits, ("user", "edge"), scatter_dimension=0, tiled=True),
    )
    share_rows = item_sum.shape[0]
    position = lax.axis_index("user") * edge_count + lax.axis_index("edge")
    own_items = lax.dynamic_slice_in_dim(item_emb, position * share_rows, share_rows, 0)
    merged = own_items.astype(jnp.float32) + item_sum / jnp.maximum(item_degree, 1.0)[:, None]
    hidden = jax.nn.silu(
        jnp.dot(merged.astype(jnp.bfloat16), up_weight, preferred_element_type=jnp.float32)
    ).astype(jnp.bfloat16)
    return (merged + jnp.dot(hidden, down_weight, preferred_element_type=jnp.float32)).astype(
        jnp.bfloat16
    )


def solution(mesh):
    return jax.shard_map(
        body,
        mesh=mesh,
        in_specs=(
            P("item", None),
            P("user", None),
            P("item", "user", "edge", None),
            P("item", "user", "edge", None),
            P("item", "user", "edge", None, None),
            P("item", "user", "edge"),
            P(),
            P(),
            P(),
        ),
        out_specs=P(("item", "user", "edge"), None),
        check_vma=False,
    )
```

profile of v0, /device:TPU:8, one launch (start us, length us, event | category | flops | bytes accessed | tf_op | source)
XLA Modules:
  0.0 323.8 jit_solution(14199632267870395044)
XLA Ops:
  7.3 3.4 %broadcast_in_dim.57 = f32[48,128,256]{2,0,1:T(8,128)} broadcast(f32[]{:T(128)} %constant.89.clone.1), dimensions={} | broadcast | bytes 6291460 | tf_op jit(solution)/shard_map/broadcast_in_dim | solution.py:66
  10.8 48.7 %while.26 = (s32[]{:T(128)}, f32[48,128,256]{2,0,1:T(8,128)}, f32[48,128]{1,0:T(8,128)S(1)}, s32[]{:T(128)}, s32[96]{0:T(128)S(1)}, /*index=5*/s32[96,128]{1,0:T...) while((s32[]{:T(128)}, f32[48,128,256]{2,0,1:T(8,128)}, ...), condition=%wide.region_2.3_spmd.clone, body=%wide.region_0.2_spmd.clone.sunk | while | flops 881072384 | bytes 77747608 | solution.py:69
  10.8 0.7 compare_and_fusion.4
  11.5 2.3 gather_fusion
  13.8 0.8 fusion.79
  14.7 1.9 copy-done.1
  16.6 6.5 %fusion.80 = f32[48,128,256]{2,0,1:T(8,128)S(1)} fusion(f32[48,128,256]{2,0,1:T(8,128)S(1)} %copy-done.1, f32[32,128,256]{2,1,0:T(8,128)S(1)} %fusion.79, s32[32]{0:T(128)S(1)} %dynamic_slice.44), kind=kOutput, calls=%fused_computation.6.clone.1 | convolution fusion | flops 605554176 | bytes 16777344 | tf_op jit(solution)/shard_map/while/body/sg,gcd->scd/dot_general | solution.py:58
  23.1 2.6 copy-done.2
  25.8 0.9 convert_reduce_fusion.4
  26.9 0.7 compare_and_fusion.4
  27.7 2.3 gather_fusion
  30.0 0.8 fusion.79
  30.9 1.9 copy-done.1
  32.7 6.5 %fusion.80 = f32[48,128,256]{2,0,1:T(8,128)S(1)} fusion(f32[48,128,256]{2,0,1:T(8,128)S(1)} %copy-done.1, f32[32,128,256]{2,1,0:T(8,128)S(1)} %fusion.79, s32[32]{0:T(128)S(1)} %dynamic_slice.44), kind=kOutput, calls=%fused_computation.6.clone.1 | convolution fusion | flops 605554176 | bytes 16777344 | tf_op jit(solution)/shard_map/while/body/sg,gcd->scd/dot_general | solution.py:58
  39.3 2.6 copy-done.2
  41.9 0.9 convert_reduce_fusion.4
  43.1 0.7 compare_and_fusion.4
  43.8 2.3 gather_fusion
  46.1 0.8 fusion.79
  47.0 1.9 copy-done.1
  48.9 6.5 %fusion.80 = f32[48,128,256]{2,0,1:T(8,128)S(1)} fusion(f32[48,128,256]{2,0,1:T(8,128)S(1)} %copy-done.1, f32[32,128,256]{2,1,0:T(8,128)S(1)} %fusion.79, s32[32]{0:T(128)S(1)} %dynamic_slice.44), kind=kOutput, calls=%fused_computation.6.clone.1 | convolution fusion | flops 605554176 | bytes 16777344 | tf_op jit(solution)/shard_map/while/body/sg,gcd->scd/dot_general | solution.py:58
  55.5 2.6 copy-done.2
  58.1 0.9 convert_reduce_fusion.4
  59.4 9.1 %copy.15 = f32[48,128,256]{2,1,0:T(8,128)} copy(f32[48,128,256]{2,0,1:T(8,128)} %get-tuple-element.113) | data formatting | bytes 12582912 | tf_op jit(solution)/shard_map/while | solution.py:69
  68.6 124.2 %psum.15 = f32[6144]{0:T(1024)S(1)} all-reduce(f32[6144]{0:T(1024)S(1)} %bitcast.34), channel_id=1, replica_groups=mesh['item'=16,'user'=8,'edge'=2] {'item','edge'}, use_global_device_ids=true, to_apply=%region_4.5 | all-reduce | flops 6144 | bytes 49152 | tf_op jit(solution)/shard_map/psum | solution.py:72
  192.8 3.7 %all-reduce.3.cloned.1.call-done = f32[6144,256]{1,0:T(8,128)} async-done(((f32[6144,256]{1,0:T(8,128)}), f32[6144,256]{1,0:T(8,128)}) %all-reduce.3.cloned.1.call-update) | async-done | bytes 6291472 | tf_op jit(solution)/shard_map/psum | solution.py:72
  196.5 6.1 %add_convert_fusion = bf16[6144,256]{1,0:T(8,128)(2,1)} fusion(bf16[6144,256]{1,0:T(8,128)(2,1)} %param.14, bf16[256,256]{1,0:T(8,128)(2,1)S(1)} %copy-done.9, f32[6144,256]{1,0:T(8,128)} %all-reduce.3.cloned.1.call-done, f32[6144]{0:T(1024)S(1)} %broadcast_maximum_fusion), kind=kOutput, calls=%fused_computation.51 | convolution fusion | flops 819462144 | bytes 12738560 | tf_op jit(solution)/shard_map/dot_general | solution.py:11
  202.6 2.5 broadcast_in_dim.55
  205.1 39.7 %while.27 = (s32[]{:T(128)}, f32[32,128,256]{2,0,1:T(8,128)}, f32[32]{0:T(128)S(1)}, s32[]{:T(128)}, s32[96]{0:T(128)S(1)}, /*index=5*/s32[]{:T(128)}, s32[96,12...) while((s32[]{:T(128)}, f32[32,128,256]{2,0,1:T(8,128)}, ...), condition=%wide.region_7.8_spmd.clone, body=%wide.region_5.7_spmd.clone.sunk | while | flops 674241792 | bytes 56678324 | solution.py:94
  205.1 0.7 compare_and_fusion.5
  205.8 2.6 gather_fusion.1
  208.4 2.5 fusion.85
  211.0 5.1 %fusion.86 = f32[32,128,256]{2,0,1:T(8,128)S(1)} fusion(f32[32,128,256]{2,0,1:T(8,128)S(1)} %copy-done.3, f32[32,128,256]{2,1,0:T(8,128)S(1)} %fusion.85, s32[32]{0:T(128)S(1)} %dynamic_slice.46, pred[32]{0:T(512)(128)(4,1)S(1)} %get-tuple-element.324), kind=kOutput, calls=%fused_computation.30.clone.1 | convolution fusion | flops 403703808 | bytes 12583072 | tf_op jit(solution)/shard_map/while/body/sg,grd->srd/dot_general | solution.py:84
  216.1 2.0 copy-done.4
  218.2 0.7 compare_and_fusion.5
  218.9 2.6 gather_fusion.1
  221.6 2.5 fusion.85
  224.1 5.1 %fusion.86 = f32[32,128,256]{2,0,1:T(8,128)S(1)} fusion(f32[32,128,256]{2,0,1:T(8,128)S(1)} %copy-done.3, f32[32,128,256]{2,1,0:T(8,128)S(1)} %fusion.85, s32[32]{0:T(128)S(1)} %dynamic_slice.46, pred[32]{0:T(512)(128)(4,1)S(1)} %get-tuple-element.324), kind=kOutput, calls=%fused_computation.30.clone.1 | convolution fusion | flops 403703808 | bytes 12583072 | tf_op jit(solution)/shard_map/while/body/sg,grd->srd/dot_general | solution.py:84
  229.3 2.0 copy-done.4
  231.4 0.7 compare_and_fusion.5
  232.1 2.6 gather_fusion.1
  234.7 2.5 fusion.85
  237.3 5.1 %fusion.86 = f32[32,128,256]{2,0,1:T(8,128)S(1)} fusion(f32[32,128,256]{2,0,1:T(8,128)S(1)} %copy-done.3, f32[32,128,256]{2,1,0:T(8,128)S(1)} %fusion.85, s32[32]{0:T(128)S(1)} %dynamic_slice.46, pred[32]{0:T(512)(128)(4,1)S(1)} %get-tuple-element.324), kind=kOutput, calls=%fused_computation.30.clone.1 | convolution fusion | flops 403703808 | bytes 12583072 | tf_op jit(solution)/shard_map/while/body/sg,grd->srd/dot_general | solution.py:84
  242.4 2.0 copy-done.4
  244.7 6.6 %copy.16 = f32[32,128,256]{2,1,0:T(8,128)} copy(f32[32,128,256]{2,0,1:T(8,128)} %get-tuple-element.115) | data formatting | bytes 8388608 | tf_op jit(solution)/shard_map/while | solution.py:94
  253.3 46.1 %all-reduce = f32[4096]{0:T(1024)S(1)} all-reduce(f32[4096]{0:T(1024)S(1)} %broadcast_bitcast_fusion), channel_id=3, replica_groups=mesh['item'=16,'user'=8,'edge'=2] {'user','edge'}, use_global_device_ids=true, to_apply=%region_9.10.clone | all-reduce | flops 4096 | bytes 32768
  299.5 15.1 %reduce-scatter.2.cloned.1.call-done = f32[256,256]{1,0:T(8,128)} async-done(((f32[4096,256]{1,0:T(8,128)}), f32[256,256]{1,0:T(8,128)}) %reduce-scatter.2.cloned.1.call-update) | async-done | bytes 262160 | tf_op jit(solution)/shard_map/reduce_scatter | solution.py:99
  314.6 2.4 fusion.43
  (66 shorter events, 3.3 us)
Async XLA Ops:
  6.5 308.0 %copy-start = (bf16[1024,256]{1,0:T(8,128)(2,1)S(1)}, bf16[1024,256]{1,0:T(8,128)(2,1)}, u32[]{:S(2)}) copy-start(bf16[1024,256]{1,0:T(8,128)(2,1)} %param.21) | copy-start | bytes 1572868
  6.5 4.2 %copy-start.7 = (s32[1,1,1,96]{3,2,1,0:T(1,128)S(1)}, s32[1,1,1,96]{3,2,1,0:T(1,128)}, u32[]{:S(2)}) copy-start(s32[1,1,1,96]{3,2,1,0:T(1,128)} %param.15) | copy-start | bytes 1156
  6.5 4.2 %copy-start.5 = (s32[1,1,1,96,128]{4,3,2,1,0:T(8,128)S(1)}, s32[1,1,1,96,128]{4,3,2,1,0:T(8,128)}, u32[]{:S(2)}) copy-start(s32[1,1,1,96,128]{4,3,2,1,0:T(8,128)} %param.17) | copy-start | bytes 147460
  6.5 4.2 %copy-start.6 = (s32[1,1,1,96]{3,2,1,0:T(1,128)S(1)}, s32[1,1,1,96]{3,2,1,0:T(1,128)}, u32[]{:S(2)}) copy-start(s32[1,1,1,96]{3,2,1,0:T(1,128)} %param.16) | copy-start | bytes 1156
  6.5 189.9 %all-reduce.3.cloned.1.call-start = ((), (), s32[]{:S(2)}) async-start(), calls=%async_computation.1 | async-start | bytes 12582912 | tf_op jit(solution)/shard_map/psum | solution.py:72
  13.8 2.8 copy-start.1
  23.1 2.6 copy-start.2
  30.0 2.8 copy-start.1
  39.3 2.6 copy-start.2
  46.1 2.8 copy-start.1
  55.4 2.6 copy-start.2
  68.5 128.0 %copy-start.9 = (bf16[256,256]{1,0:T(8,128)(2,1)S(1)}, bf16[256,256]{1,0:T(8,128)(2,1)}, u32[]{:S(2)}) copy-start(bf16[256,256]{1,0:T(8,128)(2,1)} %param.19) | copy-start | bytes 393220
  68.5 246.0 %reduce-scatter.2.cloned.1.call-start = ((), (), s32[]{:S(2)}) async-start(), calls=%async_computation.2 | async-start | bytes 4456448 | tf_op jit(solution)/shard_map/reduce_scatter | solution.py:99
  208.4 2.6 copy-start.3
  216.1 2.0 copy-start.4
  221.5 2.6 copy-start.3
  229.3 2.0 copy-start.4
  234.7 2.6 copy-start.3
  242.4 2.0 copy-start.4
  251.3 0.7 copy-start.10
  251.3 63.3 %copy-start.8 = (bf16[256,1024]{1,0:T(8,128)(2,1)S(1)}, bf16[256,1024]{1,0:T(8,128)(2,1)}, u32[]{:S(2)}) copy-start(bf16[256,1024]{1,0:T(8,128)(2,1)} %param.20) | copy-start | bytes 1572868
Sparse Core Ops, SparseCore 0:
  68.7 127.7 all-reduce.2
  251.4 63.0 reduce-scatter.1
where the time goes:
time: 325 us; the launch traced here: 324 us
  blocking collectives  170 us (52%)
  local copies, waits for them, and re-layouts  57.5 us (18%)
  matrix products  54 us (17%)
  waiting for transfers between devices  18.8 us (6%)
  between operations  14.8 us (5%)
  other arithmetic  7.42 us (2%)
    psum x1, blocking collectives, body(): whole_sum, whole_hits = lax.psum((user_part, user_hits), ('item', 'edge'))  124 us
    unnamed x1, blocking collectives  46.1 us
    dot_general x3, matrix products, first_hop(): jnp.einsum('sg,gcd->scd', chooser, contrib, precision=lax.Precision.HIGHEST)  19.6 us
    while x24, local copies, waits for them, and re-layouts  19.5 us
    dot_general x3, matrix products, second_hop(): jnp.einsum('sg,grd->srd', chooser, contrib, precision=lax.Precision.HIGHEST)  15.4 us
    reduce_scatter x1, waiting for transfers between devices, body(): lax.psum_scatter(item_part, ('user', 'edge'), scatter_dimension=0, tiled=...  15.1 us
    while x1, local copies, waits for them, and re-layouts, body(): user_part, user_hits = lax.fori_loop(0, rounds, first_hop, start)  9.08 us
    gather x3, local copies, waits for them, and re-layouts, second_hop(): gathered = jnp.take(tiled_users, users_at, axis=0)  7.71 us
  transfers between devices with their start and end apart: 2, of which 2 were waited for; matrix products, arithmetic and copies ran while one was open for 0% of the time, Pallas kernels for 0%

commit v1 on v0

v1 whole, which is shorter than its diff:
```python
import functools

import jax
import jax.numpy as jnp
from jax import lax
from jax.experimental import pallas as pl
from jax.experimental.pallas import tpu as pltpu
from jax.sharding import PartitionSpec as P

TILE = 128
MESH = pl.DeviceIdType.MESH
F32 = jnp.float32
BF16 = jnp.bfloat16
GROUP = 4
VM = pltpu.VMEM


def rows_at(offset, count, unit):
    return pl.ds(pl.multiple_of(offset, unit), count)


def mask_links(count_ref, links_ref, masked_ref):
    slot = lax.broadcasted_iota(jnp.int32, links_ref.shape, 0)
    masked_ref[...] = jnp.where(slot < count_ref[0], links_ref[...], -1)


def hop1_kernel(bi_ref, bu_ref, count_ref, links_ref, bi_row, bu_row, items_ref, part_ref, cnt_ref, hits_ref, acc, masked):
    slots = links_ref.shape[0]
    user_tiles = acc.shape[0]
    mask_links(count_ref, links_ref, masked)
    acc[...] = jnp.zeros_like(acc)

    inside = lax.broadcasted_iota(jnp.int32, (TILE, TILE), 0)

    def blocks(group, carry):
        made = []
        for k in range(GROUP):
            b = group * GROUP + k
            live = b < count_ref[0]
            it = jnp.where(live, bi_ref[b], 0)
            ut = jnp.where(live, bu_ref[b], 0)
            onehot = (masked[pl.ds(b, 1), :] == inside).astype(F32).astype(BF16)
            rows = items_ref[rows_at(it * TILE, TILE, TILE), :]
            made.append((ut, jnp.dot(onehot, rows, preferred_element_type=F32)))
        for ut, contrib in made:
            acc[ut] += contrib
        return carry

    lax.fori_loop(0, (count_ref[0] + GROUP - 1) // GROUP, blocks, 0)

    lane = lax.broadcasted_iota(jnp.int32, (slots, TILE), 1)
    column_hits = jnp.zeros((slots, TILE), F32)
    links = masked[...]
    for r in range(TILE):
        column_hits += (links[:, r : r + 1] == lane).astype(F32)
    column_hits = column_hits.astype(BF16)
    triples = user_tiles // 3
    which = lax.broadcasted_iota(jnp.int32, (triples, slots), 0) * 3
    at = bu_row[...]
    a, b, c = (
        jnp.dot((which + k == at).astype(F32).astype(BF16), column_hits, preferred_element_type=F32)
        for k in range(3)
    )
    lanes = lax.broadcasted_iota(jnp.int32, (triples, TILE), 1)
    cnt_ref[0] = a
    cnt_ref[1] = jnp.where(lanes < 32, pltpu.roll(a, 32, 1), pltpu.roll(b, 32, 1))
    cnt_ref[2] = jnp.where(lanes < 64, pltpu.roll(b, 64, 1), pltpu.roll(c, 64, 1))
    cnt_ref[3] = pltpu.roll(c, 96, 1)

    slot = lax.broadcasted_iota(jnp.int32, (TILE, slots), 1)
    tile = lax.broadcasted_iota(jnp.int32, (TILE, slots), 0)
    chosen = ((tile == bi_row[...]) & (slot < count_ref[0])).astype(F32).astype(BF16)
    ones = jnp.ones((8, slots), BF16)
    hits_ref[...] = lax.dot_general(ones, chosen, (((1,), (1,)), ((), ())), preferred_element_type=F32)

    def store(t, carry):
        part_ref[rows_at(t * TILE, TILE, TILE), :] = acc[t].astype(BF16)
        return carry

    lax.fori_loop(0, user_tiles, store, 0)


def hop2_kernel(bi_ref, bu_ref, count_ref, links_ref, users_ref, part_ref, acc, masked):
    mask_links(count_ref, links_ref, masked)
    acc[...] = jnp.zeros_like(acc)
    inside = lax.broadcasted_iota(jnp.int32, (TILE, TILE), 0)

    def blocks(group, carry):
        made = []
        for k in range(GROUP):
            b = group * GROUP + k
            live = b < count_ref[0]
            it = jnp.where(live, bi_ref[b], 0)
            ut = jnp.where(live, bu_ref[b], 0)
            onehot = (masked[pl.ds(b, 1), :] == inside).astype(F32).astype(BF16)
            rows = users_ref[rows_at(ut * TILE, TILE, TILE), :]
            contrib = lax.dot_general(onehot, rows, (((0,), (0,)), ((), ())), preferred_element_type=F32)
            made.append((it, contrib))
        for it, contrib in made:
            acc[it] += contrib
        return carry

    lax.fori_loop(0, (count_ref[0] + GROUP - 1) // GROUP, blocks, 0)

    def store(t, carry):
        part_ref[rows_at(t * TILE, TILE, TILE), :] = acc[t].astype(BF16)
        return carry

    lax.fori_loop(0, acc.shape[0], store, 0)


class Wires:
    def __init__(self, send_sem, recv_sem):
        self.send_sem, self.recv_sem, self.made = send_sem, recv_sem, []

    def start(self, src, dst, device):
        at = len(self.made)
        copy = pltpu.make_async_remote_copy(
            src_ref=src,
            dst_ref=dst,
            send_sem=self.send_sem.at[at],
            recv_sem=self.recv_sem.at[at],
            device_id=device,
            device_id_type=MESH,
        )
        copy.start()
        self.made.append(copy)
        return copy

    def finish(self):
        for copy in self.made:
            copy.wait_send()


def enter(peers):
    barrier = pltpu.get_barrier_semaphore()
    for peer in peers:
        pl.semaphore_signal(barrier, inc=1, device_id=peer, device_id_type=MESH)
    pl.semaphore_wait(barrier, len(peers))


def up(x):
    return x.astype(F32)


SIDE = 4
PLANE_COPIES = 111


def plane_kernel(
    part, cnt, emb, weight, users, from_core, sums, opposite, final, total, opposite2, final2, small, total_cnt, got_cnt,
    own_rows, local_sem, send_sem, recv_sem,
):
    item, e = lax.axis_index("item"), lax.axis_index("edge")
    x, y = item // SIDE, item % SIDE
    seg = part.shape[0] // (2 * 2 * SIDE * SIDE)
    block = SIDE * seg
    half, half2 = block // 2, seg // 2

    def step(value, by):
        return lax.rem(value + (by + SIDE), SIDE)

    def along_x(by):
        return {"item": step(x, by) * SIDE + y}

    def along_y(by):
        return {"item": x * SIDE + step(y, by)}

    other = {"edge": 1 - e}
    p1, p2 = (x, y), (y, x)
    ring1, ring2 = (along_x, along_y), (along_y, along_x)

    def block_at(core, h, k1):
        return ((core * 2 + h) * SIDE + step(p1[h], k1)) * block

    def seg_at(core, h, k1, k2):
        return block_at(core, h, k1) + step(p2[h], k2) * seg

    own_copies = []
    for h in range(2):
        copy = pltpu.make_async_copy(
            emb.at[rows_at(seg_at(e, h, 0, 0), seg, seg)], own_rows.at[h], local_sem.at[h]
        )
        copy.start()
        own_copies.append(copy)

    enter([along_x(1), along_x(-1), along_y(1), along_y(-1), other])
    w = Wires(send_sem, recv_sem)

    core_cnt = w.start(cnt, got_cnt.at[0], other)
    core_sums = {}
    for k in (2, 1, 3, 0):
        for h in range(2):
            core_sums[h, k] = w.start(
                part.at[rows_at(block_at(1 - e, h, k), block, seg)], from_core.at[h, k], other
            )

    def mine(h, k, start, size):
        return up(part[rows_at(block_at(e, h, k) + start, size, half2), :]) + up(from_core[h, k, pl.ds(start, size), :])

    to_far = {}
    for h in range(2):
        core_sums[h, 2].wait_recv()
        sums[h, 2] = mine(h, 2, 0, block).astype(BF16)
        to_far[h, 1] = w.start(sums.at[h, 2, pl.ds(0, half)], opposite.at[h, 0], ring1[h](1))
        to_far[h, -1] = w.start(sums.at[h, 2, pl.ds(half, half)], opposite.at[h, 1], ring1[h](-1))
    near = {}
    for h in range(2):
        core_sums[h, 1].wait_recv()
        sums[h, 1, pl.ds(half, half)] = mine(h, 1, half, half).astype(BF16)
        near[h, 1, 0] = w.start(sums.at[h, 1, pl.ds(half, half)], final.at[h, 0, pl.ds(half, half)], ring1[h](1))
        core_sums[h, 3].wait_recv()
        sums[h, 3, pl.ds(0, half)] = mine(h, 3, 0, half).astype(BF16)
        near[h, -1, 0] = w.start(sums.at[h, 3, pl.ds(0, half)], final.at[h, 1, pl.ds(0, half)], ring1[h](-1))
    core_cnt.wait_recv()
    total_cnt[0] = cnt[...] + got_cnt[0]
    cnt_x = [w.start(total_cnt.at[0], got_cnt.at[1], along_x(1)), w.start(total_cnt.at[0], got_cnt.at[2], along_x(-1))]
    for h in range(2):
        to_far[h, 1].wait_recv()
        sums[h, 1, pl.ds(0, half)] = (mine(h, 1, 0, half) + up(opposite[h, 0])).astype(BF16)
        near[h, 1, 1] = w.start(sums.at[h, 1, pl.ds(0, half)], final.at[h, 0, pl.ds(0, half)], ring1[h](1))
        to_far[h, -1].wait_recv()
        sums[h, 3, pl.ds(half, half)] = (mine(h, 3, half, half) + up(opposite[h, 1])).astype(BF16)
        near[h, -1, 1] = w.start(sums.at[h, 3, pl.ds(half, half)], final.at[h, 1, pl.ds(half, half)], ring1[h](-1))
    cnt_x[0].wait_recv()
    cnt_x.append(w.start(got_cnt.at[1], got_cnt.at[3], along_x(1)))
    for h in range(2):
        core_sums[h, 0].wait_recv()
        near[h, 1, 0].wait_recv()
        near[h, -1, 0].wait_recv()
        total[h, pl.ds(0, half)] = mine(h, 0, 0, half) + up(final[h, 1, pl.ds(0, half)])
        total[h, pl.ds(half, half)] = mine(h, 0, half, half) + up(final[h, 0, pl.ds(half, half)])
    cnt_x[1].wait_recv()
    cnt_x[2].wait_recv()
    total_cnt[1] = total_cnt[0] + got_cnt[1] + got_cnt[2] + got_cnt[3]
    cnt_y = [w.start(total_cnt.at[1], got_cnt.at[4], along_y(1)), w.start(total_cnt.at[1], got_cnt.at[5], along_y(-1))]

    def ready(h, k, start, size):
        return total[h, rows_at(step(p2[h], k) * seg + start, size, half2), :]

    to_far2, near2 = {}, {}
    for h in range(2):
        near[h, 1, 1].wait_recv()
        near[h, -1, 1].wait_recv()
        total[h, pl.ds(0, half)] += up(final[h, 0, pl.ds(0, half)])
        total[h, pl.ds(half, half)] += up(final[h, 1, pl.ds(half, half)])
        small[h, 0] = ready(h, 2, 0, seg).astype(BF16)
        to_far2[h, 1] = w.start(small.at[h, 0, pl.ds(0, half2)], opposite2.at[h, 0], ring2[h](1))
        to_far2[h, -1] = w.start(small.at[h, 0, pl.ds(half2, half2)], opposite2.at[h, 1], ring2[h](-1))
        small[h, 1, pl.ds(half2, half2)] = ready(h, 1, half2, half2).astype(BF16)
        near2[h, 1, 0] = w.start(small.at[h, 1, pl.ds(half2, half2)], final2.at[h, 0, pl.ds(half2, half2)], ring2[h](1))
        small[h, 2, pl.ds(0, half2)] = ready(h, -1, 0, half2).astype(BF16)
        near2[h, -1, 0] = w.start(small.at[h, 2, pl.ds(0, half2)], final2.at[h, 1, pl.ds(0, half2)], ring2[h](-1))
    cnt_y[0].wait_recv()
    cnt_y.append(w.start(got_cnt.at[4], got_cnt.at[6], along_y(1)))
    for h in range(2):
        to_far2[h, 1].wait_recv()
        small[h, 1, pl.ds(0, half2)] = (ready(h, 1, 0, half2) + up(opposite2[h, 0])).astype(BF16)
        near2[h, 1, 1] = w.start(small.at[h, 1, pl.ds(0, half2)], final2.at[h, 0, pl.ds(0, half2)], ring2[h](1))
        to_far2[h, -1].wait_recv()
        small[h, 2, pl.ds(half2, half2)] = (ready(h, -1, half2, half2) + up(opposite2[h, 1])).astype(BF16)
        near2[h, -1, 1] = w.start(small.at[h, 2, pl.ds(half2, half2)], final2.at[h, 1, pl.ds(half2, half2)], ring2[h](-1))
    cnt_y[1].wait_recv()
    cnt_y[2].wait_recv()
    total_cnt[2] = total_cnt[1] + got_cnt[4] + got_cnt[5] + got_cnt[6]

    own_diag = lax.broadcasted_iota(jnp.int32, (seg, TILE), 0) == lax.broadcasted_iota(jnp.int32, (seg, TILE), 1)
    for h in range(2):
        degree = total_cnt[2, step(p2[h], 0), pl.ds((e * 2 + h) * SIDE + p1[h], 1), :]
        degree = jnp.sum(jnp.where(own_diag, jnp.broadcast_to(degree, (seg, TILE)), 0.0), axis=1, keepdims=True)
        own_copies[h].wait()
        for s in (1, -1):
            near2[h, s, 0].wait_recv()
            near2[h, s, 1].wait_recv()
        summed = ready(h, 0, 0, seg) + up(final2[h, 0]) + up(final2[h, 1])
        average = (summed / jnp.maximum(degree, 1.0)).astype(BF16)
        v = jnp.dot(average, weight[...], preferred_element_type=F32)
        fresh = up(own_rows[h]) + v / (1.0 + jnp.exp(-v))
        users[rows_at(seg_at(e, h, 0, 0), seg, seg), :] = fresh.astype(BF16)

    def send(h, k1, k2, start, size, device):
        there = users.at[rows_at(seg_at(e, h, k1, k2) + start, size, half2)]
        return w.start(there, there, device)

    c1, c1f, c2, c2f, d = {}, {}, {}, {}, []

    def spread(h, k2):
        for s in (1, -1):
            c2[h, k2, s] = send(h, 0, k2, 0, seg, ring1[h](s))
        d.append(send(h, 0, k2, 0, seg, other))

    def relay(h, k2):
        c2[h, k2, 1].wait_recv()
        c2f[h, k2, 1] = send(h, -1, k2, 0, half2, ring1[h](1))
        d.append(send(h, -1, k2, 0, seg, other))
        c2[h, k2, -1].wait_recv()
        c2f[h, k2, -1] = send(h, 1, k2, half2, half2, ring1[h](-1))
        d.append(send(h, 1, k2, 0, seg, other))

    for h in range(2):
        for s in (1, -1):
            c1[h, s] = send(h, 0, 0, 0, seg, ring2[h](s))
        spread(h, 0)
    for h in range(2):
        c1[h, 1].wait_recv()
        c1f[h, 1] = send(h, 0, -1, 0, half2, ring2[h](1))
        c1[h, -1].wait_recv()
        c1f[h, -1] = send(h, 0, 1, half2, half2, ring2[h](-1))
        spread(h, -1)
        spread(h, 1)
    for h in range(2):
        relay(h, 0)
    for h in range(2):
        c1f[h, 1].wait_recv()
        c1f[h, -1].wait_recv()
        spread(h, 2)
    for k2 in (-1, 1, 2):
        for h in range(2):
            relay(h, k2)
    for k2 in (0, -1, 1, 2):
        for h in range(2):
            c2f[h, k2, 1].wait_recv()
            c2f[h, k2, -1].wait_recv()
            d.append(send(h, 2, k2, 0, seg, other))
    for copy in d:
        copy.wait_recv()
    w.finish()
    assert len(w.made) <= PLANE_COPIES, len(w.made)


DEPTH = 8
COLUMN_COPIES = 8 + 14 + 8


def column_kernel(
    part, hits, items, up_weight, down_weight, out, from_core, sums, got_up, got_down, chip_hits, got_hits, own_rows, up_v,
    down_v, local_sem, send_sem, recv_sem,
):
    u, e = lax.axis_index("user"), lax.axis_index("edge")
    share = out.shape[0]
    half = share // 2

    def step(by):
        return lax.rem(u + (by + DEPTH), DEPTH)

    other = {"edge": 1 - e}
    place = {1: {"user": step(1)}, -1: {"user": step(-1)}}

    def chunk(k, core):
        return (step(k) * 2 + core) * share

    local = [
        pltpu.make_async_copy(items.at[rows_at(chunk(0, e), share, share)], own_rows, local_sem.at[0]),
        pltpu.make_async_copy(up_weight, up_v, local_sem.at[1]),
        pltpu.make_async_copy(down_weight, down_v, local_sem.at[2]),
    ]
    for copy in local:
        copy.start()
    enter([place[1], place[-1], other])
    w = Wires(send_sem, recv_sem)
    core_hits = w.start(hits, got_hits.at[0], other)
    core = {}
    for k in (4, 3, -3, 2, -2, 1, -1, 0):
        core[k] = w.start(part.at[rows_at(chunk(k, 1 - e), share, share)], from_core.at[k % DEPTH], other)

    def mine(k, q):
        return up(part[rows_at(chunk(k, e) + q * half, half, half), :]) + up(from_core[k % DEPTH, pl.ds(q * half, half), :])

    got = {1: got_up, -1: got_down}
    wires = {}
    hit_wires = {}

    landed = set()

    def land(k):
        if k not in landed:
            landed.add(k)
            core[k].wait_recv()

    def pass_on(s, k, q):
        land(4 if k == 4 else s * k)
        value = mine(s * k, q)
        if (s, k + 1, q) in wires:
            wires[s, k + 1, q].wait_recv()
            value += up(got[s][k, q])
        running = (s * k) % DEPTH, pl.ds(q * half, half)
        sums[running] = value.astype(BF16)
        wires[s, k, q] = w.start(sums.at[running], got[s].at[k - 1, q], place[s])

    for k in (4, 3):
        for s in (1, -1):
            pass_on(s, k, int((s == 1) == (k == 3)))
    core_hits.wait_recv()
    chip_hits[...] = hits[...] + got_hits[0]
    for s in (1, -1):
        hit_wires[s, 1] = w.start(chip_hits, got_hits.at[1 if s == 1 else 5], place[s])
    for k in (3, 2, 1):
        for s, q in ((1, 0), (-1, 1)):
            pass_on(s, k, q)
        far = 5 - k
        for s in (1, -1):
            hit_wires[s, far - 1].wait_recv()
            if s == 1 or far < 4:
                base = 1 if s == 1 else 5
                hit_wires[s, far] = w.start(got_hits.at[base + far - 2], got_hits.at[base + far - 1], place[s])
        if k > 1:
            for s, q in ((1, 1), (-1, 0)):
                pass_on(s, k - 1, q)
    hit_wires[1, 4].wait_recv()
    land(0)
    degree = chip_hits[...]
    for k in range(1, DEPTH):
        degree += got_hits[k]
    lane = lax.broadcasted_iota(jnp.int32, degree.shape, 1)
    for copy in local:
        copy.wait()
    for q in range(2):
        wires[1, 1, q].wait_recv()
        wires[-1, 1, q].wait_recv()
    for q in range(2):
        summed = mine(0, q) + up(got_up[0, q]) + up(got_down[0, q])
        mine_only = jnp.where(lane == (u * 2 + e) * 2 + q, degree, 0.0)
        own_degree = jnp.sum(mine_only[0:1, :], axis=1, keepdims=True)
        merged = up(own_rows[pl.ds(q * half, half), :]) + summed / jnp.maximum(own_degree, 1.0)
        v = jnp.dot(merged.astype(BF16), up_v[...], preferred_element_type=F32)
        hidden = (v / (1.0 + jnp.exp(-v))).astype(BF16)
        out[pl.ds(q * half, half), :] = (merged + jnp.dot(hidden, down_v[...], preferred_element_type=F32)).astype(BF16)
    w.finish()
    assert len(w.made) <= COLUMN_COPIES, len(w.made)


def vmem():
    return pl.BlockSpec(memory_space=VM)


def smem():
    return pl.BlockSpec(memory_space=pltpu.SMEM)


def hbm():
    return pl.BlockSpec(memory_space=pl.ANY)


def hop1(bi, bu, count, links, items, user_rows):
    slots, channels = links.shape[0], items.shape[1]
    return pl.pallas_call(
        hop1_kernel,
        out_shape=(
            jax.ShapeDtypeStruct((user_rows, channels), BF16),
            jax.ShapeDtypeStruct((SIDE, user_rows // (3 * TILE), TILE), F32),
            jax.ShapeDtypeStruct((8, TILE), F32),
        ),
        in_specs=[smem(), smem(), smem(), vmem(), vmem(), vmem(), vmem()],
        out_specs=(vmem(), vmem(), vmem()),
        scratch_shapes=[VM((user_rows // TILE, TILE, channels), F32), VM((slots, TILE), jnp.int32)],
        compiler_params=pltpu.CompilerParams(vmem_limit_bytes=32 * 2**20),
        name="hop1",
    )(bi, bu, count, links, bi.reshape(1, slots), bu.reshape(1, slots), items)


def hop2(bi, bu, count, links, users, item_rows):
    slots, channels = links.shape[0], users.shape[1]
    return pl.pallas_call(
        hop2_kernel,
        out_shape=jax.ShapeDtypeStruct((item_rows, channels), BF16),
        in_specs=[smem(), smem(), smem(), vmem(), vmem()],
        out_specs=vmem(),
        scratch_shapes=[VM((item_rows // TILE, TILE, channels), F32), VM((slots, TILE), jnp.int32)],
        compiler_params=pltpu.CompilerParams(vmem_limit_bytes=32 * 2**20),
        name="hop2",
    )(bi, bu, count, links, users)


def plane(part, cnt, emb, weight):
    rows, channels = part.shape
    seg = rows // (4 * SIDE * SIDE)
    block = SIDE * seg
    return pl.pallas_call(
        plane_kernel,
        out_shape=jax.ShapeDtypeStruct((rows, channels), BF16),
        in_specs=[vmem(), vmem(), hbm(), vmem()],
        out_specs=vmem(),
        scratch_shapes=[
            VM((2, SIDE, block, channels), BF16),
            VM((2, SIDE, block, channels), BF16),
            VM((2, 2, block // 2, channels), BF16),
            VM((2, 2, block, channels), BF16),
            VM((2, block, channels), F32),
            VM((2, 2, seg // 2, channels), BF16),
            VM((2, 2, seg, channels), BF16),
            VM((2, 3, seg, channels), BF16),
            VM((3,) + cnt.shape, F32),
            VM((7,) + cnt.shape, F32),
            VM((2, seg, channels), BF16),
            pltpu.SemaphoreType.DMA((2,)),
            pltpu.SemaphoreType.DMA((PLANE_COPIES,)),
            pltpu.SemaphoreType.DMA((PLANE_COPIES,)),
        ],
        compiler_params=pltpu.CompilerParams(collective_id=0, has_side_effects=True, vmem_limit_bytes=32 * 2**20),
        name="plane",
    )(part, cnt, emb, weight)


def column(part, hits, items, up_weight, down_weight):
    rows, channels = part.shape
    share = rows // (2 * DEPTH)
    return pl.pallas_call(
        column_kernel,
        out_shape=jax.ShapeDtypeStruct((share, channels), BF16),
        in_specs=[vmem(), vmem(), hbm(), hbm(), hbm()],
        out_specs=vmem(),
        scratch_shapes=[
            VM((DEPTH, share, channels), BF16),
            VM((DEPTH, share, channels), BF16),
            VM((4, 2, share // 2, channels), BF16),
            VM((4, 2, share // 2, channels), BF16),
            VM(hits.shape, F32),
            VM((DEPTH,) + hits.shape, F32),
            VM((share, channels), BF16),
            VM(up_weight.shape, BF16),
            VM(down_weight.shape, BF16),
            pltpu.SemaphoreType.DMA((3,)),
            pltpu.SemaphoreType.DMA((COLUMN_COPIES,)),
            pltpu.SemaphoreType.DMA((COLUMN_COPIES,)),
        ],
        compiler_params=pltpu.CompilerParams(collective_id=1, has_side_effects=True, vmem_limit_bytes=32 * 2**20),
        name="column",
    )(part, hits, items, up_weight, down_weight)


def body(item_emb, user_emb, block_item, block_user, block_rows, block_count, user_weight, up_weight, down_weight):
    bi, bu, count = block_item.reshape(-1), block_user.reshape(-1), block_count.reshape(-1)
    links = block_rows.reshape(-1, TILE)
    user_part, cnt, hits = hop1(bi, bu, count, links, item_emb, user_emb.shape[0])
    users = plane(user_part, cnt, user_emb, user_weight)
    item_part = hop2(bi, bu, count, links, users, item_emb.shape[0])
    return column(item_part, hits, item_emb, up_weight, down_weight)


def solution(mesh):
    return jax.shard_map(
        body,
        mesh=mesh,
        in_specs=(
            P("item", None),
            P("user", None),
            P("item", "user", "edge", None),
            P("item", "user", "edge", None),
            P("item", "user", "edge", None, None),
            P("item", "user", "edge"),
            P(),
            P(),
            P(),
        ),
        out_specs=P(("item", "user", "edge"), None),
        check_vma=False,
    )
```

time: 325 us -> 87.5 us (0.27)
  blocking collectives: 170 us -> 0 us
  Pallas kernels: 0 us -> 78.8 us
  matrix products: 54 us -> 0 us
  local copies, waits for them, and re-layouts: 57.5 us -> 7.16 us
  waiting for transfers between devices: 18.8 us -> 0 us
  between operations: 14.8 us -> 0.75 us
  other arithmetic: 7.42 us -> 0 us
    psum x1 -> x0, blocking collectives: 124 us -> none  [body(): whole_sum, whole_hits = lax.psum((user_part, user_hits), ('item', 'edge'))]
    pallas_call x0 -> x4, Pallas kernels: none -> 78.8 us  [the longest x1 42 us: plane(): pl.pallas_call(plane_kernel, out_shape=jax.ShapeDtypeStruct((rows, channe...]
    dot_general x17 -> x0, matrix products: 54 us -> none  [the longest x3 19.6 us: first_hop(): jnp.einsum('sg,gcd->scd', chooser, contrib, precision=lax.Precision.HIGHEST)]
    unnamed x1 -> x0, blocking collectives: 46.1 us -> none
    while x26 -> x0, local copies, waits for them, and re-layouts: 35.1 us -> none
    reduce_scatter x1 -> x0, waiting for transfers between devices: 15.1 us -> none  [body(): lax.psum_scatter(item_part, ('user', 'edge'), scatter_dimension=0, tiled=...]
    gather x6 -> x0, local copies, waits for them, and re-layouts: 14.5 us -> none  [the longest x3 7.71 us: second_hop(): gathered = jnp.take(tiled_users, users_at, axis=0)]
    broadcast_in_dim x4 -> x0, local copies, waits for them, and re-layouts: 5.93 us -> none  [the longest x1 3.43 us: body(): jnp.zeros((user_tiles, TILE, channels), jnp.float32)]
  transfers between devices with their start and end apart: 2 -> 0, of which waited for: 2 -> 0; matrix products, arithmetic and copies ran while one was open for 0% -> 0% of each run, Pallas kernels for 0% -> 0%
where the time goes in v1:
time: 87.5 us; the launch traced here: 86.7 us
  Pallas kernels  78.8 us (90%)
  local copies, waits for them, and re-layouts  7.16 us (8%)
    pallas_call x1, Pallas kernels, plane(): pl.pallas_call(plane_kernel, out_shape=jax.ShapeDtypeStruct((rows, channe...  42 us
    pallas_call x1, Pallas kernels, column(): pl.pallas_call(column_kernel, out_shape=jax.ShapeDtypeStruct((share, chan...  25.6 us
    unnamed x19, local copies, waits for them, and re-layouts  7.16 us
    pallas_call x1, Pallas kernels, hop1(): pl.pallas_call(hop1_kernel, out_shape=(jax.ShapeDtypeStruct((user_rows, c...  6.51 us
    pallas_call x1, Pallas kernels, hop2(): pl.pallas_call(hop2_kernel, out_shape=jax.ShapeDtypeStruct((item_rows, ch...  4.64 us

profile of v1, /device:TPU:8, one launch (start us, length us, event | category | flops | bytes accessed | tf_op | source)
XLA Modules:
  0.0 86.7 jit_solution(4916260467369439562)
XLA Ops:
  0.7 0.0 copy-start
  0.7 1.6 %copy-done = bf16[4096,256]{1,0:T(8,128)(2,1)S(1)} copy-done((bf16[4096,256]{1,0:T(8,128)(2,1)S(1)}, bf16[4096,256]{1,0:T(8,128)(2,1)}, u32[]{:S(2)}) %copy-start) | copy-done | bytes 2097176
  2.2 0.0 copy-start.5
  2.2 0.8 copy-done.5
  3.0 0.0 copy-start.7
  3.0 0.7 copy-done.7
  3.7 0.0 copy-start.8
  3.7 0.7 copy-done.8
  4.4 6.5 %hop1.1 = (bf16[6144,256]{1,0:T(8,128)(2,1)S(1)}, f32[4,16,128]{2,1,0:T(8,128)S(1)}, f32[8,128]{1,0:T(8,128)S(1)}) custom-call(s32[96]{0:T(128)S(1)} %bitcast.10, s32[96]{0:T(128)S(1)} %bitcast.13, s32[1]{0:T(128)} %bitcast.6.count_ref, s32[96,128]{1,0:T(8,128)S(1)} %bitcast.8, s32[1,96]{1,0:T(1,128)S(1)} %bitcast.11, s32[1,96]{1,0:T(1,128)S(1)} %bitcast.14, ...), custom_call_target="tpu_custom_call" | custom-call | tf_op jit(solution)/shard_map/hop1/pallas_call | solution.py:446
  10.9 0.0 copy-start.2
  10.9 1.9 %copy-done.2 = bf16[6144,256]{1,0:T(8,128)(2,1)S(1)} copy-done((bf16[6144,256]{1,0:T(8,128)(2,1)S(1)}, bf16[6144,256]{1,0:T(8,128)(2,1)}, u32[]{:S(2)}) %copy-start.2) | copy-done | bytes 3145752
  12.8 0.0 copy-start.6
  12.8 0.9 %copy-done.6 = bf16[256,256]{1,0:T(8,128)(2,1)S(1)} copy-done((bf16[256,256]{1,0:T(8,128)(2,1)S(1)}, bf16[256,256]{1,0:T(8,128)(2,1)}, u32[]{:S(2)}) %copy-start.6) | copy-done | bytes 131096
  13.7 42.0 %plane.1.users_ref = bf16[6144,256]{1,0:T(8,128)(2,1)S(1)} custom-call(bf16[6144,256]{1,0:T(8,128)(2,1)S(1)} %get-tuple-element.8.part, f32[4,16,128]{2,1,0:T(8,128)S(1)} %get-tuple-element.9.cnt, bf16[6144,256]{1,0:T(8,128)(2,1)S(1)} %copy-done.2, bf16[256,256]{1,0:T(8,128)(2,1)S(1)} %copy-done.6), custom_call_target="tpu_custom_call" | custom-call | tf_op jit(solution)/shard_map/plane/pallas_call | solution.py:478
  55.7 0.0 copy-start.1
  55.7 0.0 copy-start.3
  55.7 0.0 copy-start.4
  55.8 4.6 %hop2.1.part = bf16[4096,256]{1,0:T(8,128)(2,1)S(1)} custom-call(s32[96]{0:T(128)S(1)} %bitcast.12, s32[96]{0:T(128)S(1)} %bitcast.15, s32[1]{0:T(128)} %bitcast.7.count_ref, s32[96,128]{1,0:T(8,128)S(1)} %bitcast.9, bf16[6144,256]{1,0:T(8,128)(2,1)S(1)} %plane.1.users_ref), custom_call_target="tpu_custom_call" | custom-call | tf_op jit(solution)/shard_map/hop2/pallas_call | solution.py:463
  60.4 0.0 copy-done.1
  60.4 0.0 copy-done.3
  60.4 0.0 copy-done.4
  60.4 25.6 %column.1 = bf16[256,256]{1,0:T(8,128)(2,1)S(1)} custom-call(bf16[4096,256]{1,0:T(8,128)(2,1)S(1)} %hop2.1.part, f32[8,128]{1,0:T(8,128)S(1)} %get-tuple-element.10.hits, bf16[4096,256]{1,0:T(8,128)(2,1)S(1)} %copy-done.1, bf16[256,1024]{1,0:T(8,128)(2,1)S(1)} %copy-done.3, bf16[1024,256]{1,0:T(8,128)(2,1)S(1)} %copy-done.4), custom_call_target="tpu_custom_call" | custom-call | tf_op jit(solution)/shard_map/column/pallas_call | solution.py:507
  86.0 0.7 copy.12
Async XLA Ops:
  0.7 1.6 %copy-start = (bf16[4096,256]{1,0:T(8,128)(2,1)S(1)}, bf16[4096,256]{1,0:T(8,128)(2,1)}, u32[]{:S(2)}) copy-start(bf16[4096,256]{1,0:T(8,128)(2,1)} %items.1) | copy-start | bytes 6291460
  2.2 0.8 copy-start.5
  3.0 0.7 copy-start.7
  3.7 0.7 copy-start.8
  10.9 1.9 %copy-start.2 = (bf16[6144,256]{1,0:T(8,128)(2,1)S(1)}, bf16[6144,256]{1,0:T(8,128)(2,1)}, u32[]{:S(2)}) copy-start(bf16[6144,256]{1,0:T(8,128)(2,1)} %emb.1) | copy-start | bytes 9437188
  12.8 0.9 %copy-start.6 = (bf16[256,256]{1,0:T(8,128)(2,1)S(1)}, bf16[256,256]{1,0:T(8,128)(2,1)}, u32[]{:S(2)}) copy-start(bf16[256,256]{1,0:T(8,128)(2,1)} %weight.1) | copy-start | bytes 393220
  55.7 4.7 %copy-start.1 = (bf16[4096,256]{1,0:T(8,128)(2,1)S(1)}, bf16[4096,256]{1,0:T(8,128)(2,1)}, u32[]{:S(2)}) copy-start(bf16[4096,256]{1,0:T(8,128)(2,1)} %items.1) | copy-start | bytes 6291460
  55.7 4.7 %copy-start.3 = (bf16[256,1024]{1,0:T(8,128)(2,1)S(1)}, bf16[256,1024]{1,0:T(8,128)(2,1)}, u32[]{:S(2)}) copy-start(bf16[256,1024]{1,0:T(8,128)(2,1)} %up_weight.1) | copy-start | bytes 1572868
  55.7 4.7 %copy-start.4 = (bf16[1024,256]{1,0:T(8,128)(2,1)S(1)}, bf16[1024,256]{1,0:T(8,128)(2,1)}, u32[]{:S(2)}) copy-start(bf16[1024,256]{1,0:T(8,128)(2,1)} %down_weight.1) | copy-start | bytes 1572868

commit v2 on v1

--- a/solution.py
+++ b/solution.py
@@ -11,7 +11,7 @@
 MESH = pl.DeviceIdType.MESH
 F32 = jnp.float32
 BF16 = jnp.bfloat16
-GROUP = 4
+GROUP = 16
 VM = pltpu.VMEM
 
 
@@ -19,94 +19,74 @@
     return pl.ds(pl.multiple_of(offset, unit), count)
 
 
-def mask_links(count_ref, links_ref, masked_ref):
-    slot = lax.broadcasted_iota(jnp.int32, links_ref.shape, 0)
-    masked_ref[...] = jnp.where(slot < count_ref[0], links_ref[...], -1)
-
-
-def hop1_kernel(bi_ref, bu_ref, count_ref, links_ref, bi_row, bu_row, items_ref, part_ref, cnt_ref, hits_ref, acc, masked):
-    slots = links_ref.shape[0]
-    user_tiles = acc.shape[0]
-    mask_links(count_ref, links_ref, masked)
-    acc[...] = jnp.zeros_like(acc)
-
+def fetch(pairs, sems):
+    copies = [pltpu.make_async_copy(src, dst, sems.at[at]) for at, (src, dst) in enumerate(pairs)]
+    for copy in copies:
+        copy.start()
+    return copies
+
+
+def hop_blocks(from_items, bi, bu, count, links, source, acc):
     inside = lax.broadcasted_iota(jnp.int32, (TILE, TILE), 0)
+    live_count = count[0]
 
     def blocks(group, carry):
         made = []
         for k in range(GROUP):
             b = group * GROUP + k
-            live = b < count_ref[0]
-            it = jnp.where(live, bi_ref[b], 0)
-            ut = jnp.where(live, bu_ref[b], 0)
-            onehot = (masked[pl.ds(b, 1), :] == inside).astype(F32).astype(BF16)
-            rows = items_ref[rows_at(it * TILE, TILE, TILE), :]
-            made.append((ut, jnp.dot(onehot, rows, preferred_element_type=F32)))
-        for ut, contrib in made:
-            acc[ut] += contrib
+            live = b < live_count
+            it = jnp.where(live, bi[0, b], 0)
+            ut = jnp.where(live, bu[0, b], 0)
+            row = jnp.where(live, links[pl.ds(b, 1), :], -1)
+            onehot = (row == inside).astype(F32).astype(BF16)
+            if from_items:
+                rows = source[rows_at(it * TILE, TILE, TILE), :]
+                made.append((ut, jnp.dot(onehot, rows, preferred_element_type=F32)))
+            else:
+                rows = source[rows_at(ut * TILE, TILE, TILE), :]
+                made.append((it, lax.dot_general(onehot, rows, (((0,), (0,)), ((), ())), preferred_element_type=F32)))
+        for tile, contrib in made:
+            acc[rows_at(tile * TILE, TILE, TILE), :] += contrib
         return carry
 
-    lax.fori_loop(0, (count_ref[0] + GROUP - 1) // GROUP, blocks, 0)
-
-    lane = lax.broadcasted_iota(jnp.int32, (slots, TILE), 1)
-    column_hits = jnp.zeros((slots, TILE), F32)
-    links = masked[...]
-    for r in range(TILE):
-        column_hits += (links[:, r : r + 1] == lane).astype(F32)
-    column_hits = column_hits.astype(BF16)
-    triples = user_tiles // 3
+    lax.fori_loop(0, (live_count + GROUP - 1) // GROUP, blocks, 0)
+
+
+def hop1_kernel(bi_hbm, bu_hbm, count_hbm, links_hbm, items_hbm, acc, bi, bu, count, links, items, sems):
+    copies = fetch(
+        [(items_hbm, items), (links_hbm, links), (bi_hbm, bi), (bu_hbm, bu), (count_hbm, count)], sems
+    )
+    acc[...] = jnp.zeros_like(acc)
+    for copy in copies:
+        copy.wait()
+    hop_blocks(True, bi, bu, count, links, items, acc)
+
+
+def hop2_kernel(bi_hbm, bu_hbm, count_hbm, links_hbm, users, acc, bi, bu, count, links, sems):
+    copies = fetch([(links_hbm, links), (bi_hbm, bi), (bu_hbm, bu), (count_hbm, count)], sems)
+    acc[...] = jnp.zeros_like(acc)
+    for copy in copies:
+        copy.wait()
+    hop_blocks(False, bi, bu, count, links, users, acc)
+
+
+def degrees_of(cnt_ref, hits_ref, found, bi, bu, live_count):
+    slots = bu.shape[1]
+    triples = cnt_ref.shape[1]
     which = lax.broadcasted_iota(jnp.int32, (triples, slots), 0) * 3
-    at = bu_row[...]
     a, b, c = (
-        jnp.dot((which + k == at).astype(F32).astype(BF16), column_hits, preferred_element_type=F32)
-        for k in range(3)
+        jnp.dot((which + k == bu).astype(F32).astype(BF16), found, preferred_element_type=F32) for k in range(3)
     )
     lanes = lax.broadcasted_iota(jnp.int32, (triples, TILE), 1)
     cnt_ref[0] = a
     cnt_ref[1] = jnp.where(lanes < 32, pltpu.roll(a, 32, 1), pltpu.roll(b, 32, 1))
     cnt_ref[2] = jnp.where(lanes < 64, pltpu.roll(b, 64, 1), pltpu.roll(c, 64, 1))
     cnt_ref[3] = pltpu.roll(c, 96, 1)
-
     slot = lax.broadcasted_iota(jnp.int32, (TILE, slots), 1)
     tile = lax.broadcasted_iota(jnp.int32, (TILE, slots), 0)
-    chosen = ((tile == bi_row[...]) & (slot < count_ref[0])).astype(F32).astype(BF16)
+    chosen = ((tile == bi) & (slot < live_count)).astype(F32).astype(BF16)
     ones = jnp.ones((8, slots), BF16)
     hits_ref[...] = lax.dot_general(ones, chosen, (((1,), (1,)), ((), ())), preferred_element_type=F32)
-
-    def store(t, carry):
-        part_ref[rows_at(t * TILE, TILE, TILE), :] = acc[t].astype(BF16)
-        return carry
-
-    lax.fori_loop(0, user_tiles, store, 0)
-
-
-def hop2_kernel(bi_ref, bu_ref, count_ref, links_ref, users_ref, part_ref, acc, masked):
-    mask_links(count_ref, links_ref, masked)
-    acc[...] = jnp.zeros_like(acc)
-    inside = lax.broadcasted_iota(jnp.int32, (TILE, TILE), 0)
-
-    def blocks(group, carry):
-        made = []
-        for k in range(GROUP):
-            b = group * GROUP + k
-            live = b < count_ref[0]
-            it = jnp.where(live, bi_ref[b], 0)
-            ut = jnp.where(live, bu_ref[b], 0)
-            onehot = (masked[pl.ds(b, 1), :] == inside).astype(F32).astype(BF16)
-            rows = users_ref[rows_at(ut * TILE, TILE, TILE), :]
-            contrib = lax.dot_general(onehot, rows, (((0,), (0,)), ((), ())), preferred_element_type=F32)
-            made.append((it, contrib))
-        for it, contrib in made:
-            acc[it] += contrib
-        return carry
-
-    lax.fori_loop(0, (count_ref[0] + GROUP - 1) // GROUP, blocks, 0)
-
-    def store(t, carry):
-        part_ref[rows_at(t * TILE, TILE, TILE), :] = acc[t].astype(BF16)
-        return carry
-
-    lax.fori_loop(0, acc.shape[0], store, 0)
 
 
 class Wires:
@@ -148,8 +128,8 @@
 
 
 def plane_kernel(
-    part, cnt, emb, weight, users, from_core, sums, opposite, final, total, opposite2, final2, small, total_cnt, got_cnt,
-    own_rows, local_sem, send_sem, recv_sem,
+    part, bi_hbm, bu_hbm, count_hbm, links_hbm, emb, weight_hbm, users, hits, to_core, from_core, sums, opposite, final, total,
+    opposite2, final2, small, cnt, total_cnt, got_cnt, own_rows, bi, bu, count, links, weight, local_sem, send_sem, recv_sem,
 ):
     item, e = lax.axis_index("item"), lax.axis_index("edge")
     x, y = item // SIDE, item % SIDE
@@ -176,27 +156,37 @@
     def seg_at(core, h, k1, k2):
         return block_at(core, h, k1) + step(p2[h], k2) * seg
 
-    own_copies = []
-    for h in range(2):
-        copy = pltpu.make_async_copy(
-            emb.at[rows_at(seg_at(e, h, 0, 0), seg, seg)], own_rows.at[h], local_sem.at[h]
-        )
-        copy.start()
-        own_copies.append(copy)
-
+    own_copies = fetch(
+        [(emb.at[rows_at(seg_at(e, h, 0, 0), seg, seg)], own_rows.at[h]) for h in range(2)]
+        + [(links_hbm, links), (bi_hbm, bi), (bu_hbm, bu), (count_hbm, count), (weight_hbm, weight)],
+        local_sem,
+    )
     enter([along_x(1), along_x(-1), along_y(1), along_y(-1), other])
     w = Wires(send_sem, recv_sem)
 
-    core_cnt = w.start(cnt, got_cnt.at[0], other)
     core_sums = {}
     for k in (2, 1, 3, 0):
         for h in range(2):
-            core_sums[h, k] = w.start(
-                part.at[rows_at(block_at(1 - e, h, k), block, seg)], from_core.at[h, k], other
-            )
+            to_core[h, k] = part[rows_at(block_at(1 - e, h, k), block, seg), :].astype(BF16)
+            core_sums[h, k] = w.start(to_core.at[h, k], from_core.at[h, k], other)
+
+    for copy in own_copies[2:6]:
+        copy.wait()
+    slots = links.shape[0]
+    live = lax.broadcasted_iota(jnp.int32, (slots, TILE), 0) < count[0]
+    lane = lax.broadcasted_iota(jnp.int32, (slots, TILE), 1)
+    masked = jnp.where(live, links[...], -1)
+
+    def column_hits(first, last):
+        found = jnp.zeros((slots, TILE), F32)
+        for r in range(first, last):
+            found += (masked[:, r : r + 1] == lane).astype(F32)
+        return found
+
+    found = column_hits(0, TILE // 2)
 
     def mine(h, k, start, size):
-        return up(part[rows_at(block_at(e, h, k) + start, size, half2), :]) + up(from_core[h, k, pl.ds(start, size), :])
+        return part[rows_at(block_at(e, h, k) + start, size, half2), :] + up(from_core[h, k, pl.ds(start, size), :])
 
     to_far = {}
     for h in range(2):
@@ -212,9 +202,8 @@
         core_sums[h, 3].wait_recv()
         sums[h, 3, pl.ds(0, half)] = mine(h, 3, 0, half).astype(BF16)
         near[h, -1, 0] = w.start(sums.at[h, 3, pl.ds(0, half)], final.at[h, 1, pl.ds(0, half)], ring1[h](-1))
-    core_cnt.wait_recv()
-    total_cnt[0] = cnt[...] + got_cnt[0]
-    cnt_x = [w.start(total_cnt.at[0], got_cnt.at[1], along_x(1)), w.start(total_cnt.at[0], got_cnt.at[2], along_x(-1))]
+    degrees_of(cnt, hits, (found + column_hits(TILE // 2, TILE)).astype(BF16), bi[...], bu[...], count[0])
+    core_cnt = w.start(cnt, got_cnt.at[0], other)
     for h in range(2):
         to_far[h, 1].wait_recv()
         sums[h, 1, pl.ds(0, half)] = (mine(h, 1, 0, half) + up(opposite[h, 0])).astype(BF16)
@@ -222,14 +211,17 @@
         to_far[h, -1].wait_recv()
         sums[h, 3, pl.ds(half, half)] = (mine(h, 3, half, half) + up(opposite[h, 1])).astype(BF16)
         near[h, -1, 1] = w.start(sums.at[h, 3, pl.ds(half, half)], final.at[h, 1, pl.ds(half, half)], ring1[h](-1))
-    cnt_x[0].wait_recv()
-    cnt_x.append(w.start(got_cnt.at[1], got_cnt.at[3], along_x(1)))
+    core_cnt.wait_recv()
+    total_cnt[0] = cnt[...] + got_cnt[0]
+    cnt_x = [w.start(total_cnt.at[0], got_cnt.at[1], along_x(1)), w.start(total_cnt.at[0], got_cnt.at[2], along_x(-1))]
     for h in range(2):
         core_sums[h, 0].wait_recv()
         near[h, 1, 0].wait_recv()
         near[h, -1, 0].wait_recv()
         total[h, pl.ds(0, half)] = mine(h, 0, 0, half) + up(final[h, 1, pl.ds(0, half)])
         total[h, pl.ds(half, half)] = mine(h, 0, half, half) + up(final[h, 0, pl.ds(half, half)])
+    cnt_x[0].wait_recv()
+    cnt_x.append(w.start(got_cnt.at[1], got_cnt.at[3], along_x(1)))
     cnt_x[1].wait_recv()
     cnt_x[2].wait_recv()
     total_cnt[1] = total_cnt[0] + got_cnt[1] + got_cnt[2] + got_cnt[3]
@@ -264,11 +256,12 @@
     cnt_y[2].wait_recv()
     total_cnt[2] = total_cnt[1] + got_cnt[4] + got_cnt[5] + got_cnt[6]
 
+    for h in (0, 1, 6):
+        own_copies[h].wait()
     own_diag = lax.broadcasted_iota(jnp.int32, (seg, TILE), 0) == lax.broadcasted_iota(jnp.int32, (seg, TILE), 1)
     for h in range(2):
         degree = total_cnt[2, step(p2[h], 0), pl.ds((e * 2 + h) * SIDE + p1[h], 1), :]
         degree = jnp.sum(jnp.where(own_diag, jnp.broadcast_to(degree, (seg, TILE)), 0.0), axis=1, keepdims=True)
-        own_copies[h].wait()
         for s in (1, -1):
             near2[h, s, 0].wait_recv()
             near2[h, s, 1].wait_recv()
@@ -333,7 +326,7 @@
 
 
 def column_kernel(
-    part, hits, items, up_weight, down_weight, out, from_core, sums, got_up, got_down, chip_hits, got_hits, own_rows, up_v,
+    part, hits, items, up_weight, down_weight, out, to_core, from_core, sums, got_up, got_down, chip_hits, got_hits, own_rows, up_v,
     down_v, local_sem, send_sem, recv_sem,
 ):
     u, e = lax.axis_index("user"), lax.axis_index("edge")
@@ -361,10 +354,11 @@
     core_hits = w.start(hits, got_hits.at[0], other)
     core = {}
     for k in (4, 3, -3, 2, -2, 1, -1, 0):
-        core[k] = w.start(part.at[rows_at(chunk(k, 1 - e), share, share)], from_core.at[k % DEPTH], other)
+        to_core[k % DEPTH] = part[rows_at(chunk(k, 1 - e), share, share), :].astype(BF16)
+        core[k] = w.start(to_core.at[k % DEPTH], from_core.at[k % DEPTH], other)
 
     def mine(k, q):
-        return up(part[rows_at(chunk(k, e) + q * half, half, half), :]) + up(from_core[k % DEPTH, pl.ds(q * half, half), :])
+        return part[rows_at(chunk(k, e) + q * half, half, half), :] + up(from_core[k % DEPTH, pl.ds(q * half, half), :])
 
     got = {1: got_up, -1: got_down}
     wires = {}
@@ -438,49 +432,54 @@
 
 
 def hbm():
-    return pl.BlockSpec(memory_space=pl.ANY)
+    return pl.BlockSpec(memory_space=pltpu.HBM)
+
+
+MIB = 2**20
+
+
+def lists(slots):
+    return [pltpu.SMEM((1, slots), jnp.int32), pltpu.SMEM((1, slots), jnp.int32), pltpu.SMEM((1,), jnp.int32)]
 
 
 def hop1(bi, bu, count, links, items, user_rows):
-    slots, channels = links.shape[0], items.shape[1]
     return pl.pallas_call(
         hop1_kernel,
-        out_shape=(
-            jax.ShapeDtypeStruct((user_rows, channels), BF16),
-            jax.ShapeDtypeStruct((SIDE, user_rows // (3 * TILE), TILE), F32),
-            jax.ShapeDtypeStruct((8, TILE), F32),
-        ),
-        in_specs=[smem(), smem(), smem(), vmem(), vmem(), vmem(), vmem()],
-        out_specs=(vmem(), vmem(), vmem()),
-        scratch_shapes=[VM((user_rows // TILE, TILE, channels), F32), VM((slots, TILE), jnp.int32)],
-        compiler_params=pltpu.CompilerParams(vmem_limit_bytes=32 * 2**20),
+        out_shape=jax.ShapeDtypeStruct((user_rows, items.shape[1]), F32),
+        in_specs=[hbm()] * 5,
+        out_specs=vmem(),
+        scratch_shapes=lists(bi.shape[1])
+        + [VM(links.shape, jnp.int32), VM(items.shape, BF16), pltpu.SemaphoreType.DMA((5,))],
+        compiler_params=pltpu.CompilerParams(vmem_limit_bytes=40 * MIB),
         name="hop1",
-    )(bi, bu, count, links, bi.reshape(1, slots), bu.reshape(1, slots), items)
+    )(bi, bu, count, links, items)
 
 
 def hop2(bi, bu, count, links, users, item_rows):
-    slots, channels = links.shape[0], users.shape[1]
     return pl.pallas_call(
         hop2_kernel,
-        out_shape=jax.ShapeDtypeStruct((item_rows, channels), BF16),
-        in_specs=[smem(), smem(), smem(), vmem(), vmem()],
+        out_shape=jax.ShapeDtypeStruct((item_rows, users.shape[1]), F32),
+        in_specs=[hbm()] * 4 + [vmem()],
         out_specs=vmem(),
-        scratch_shapes=[VM((item_rows // TILE, TILE, channels), F32), VM((slots, TILE), jnp.int32)],
-        compiler_params=pltpu.CompilerParams(vmem_limit_bytes=32 * 2**20),
+        scratch_shapes=lists(bi.shape[1]) + [VM(links.shape, jnp.int32), pltpu.SemaphoreType.DMA((4,))],
+        compiler_params=pltpu.CompilerParams(vmem_limit_bytes=40 * MIB),
         name="hop2",
     )(bi, bu, count, links, users)
 
 
-def plane(part, cnt, emb, weight):
+def plane(part, bi, bu, count, links, emb, weight):
     rows, channels = part.shape
+    slots = links.shape[0]
     seg = rows // (4 * SIDE * SIDE)
     block = SIDE * seg
+    cnt = (SIDE, rows // (3 * TILE), TILE)
     return pl.pallas_call(
         plane_kernel,
-        out_shape=jax.ShapeDtypeStruct((rows, channels), BF16),
-        in_specs=[vmem(), vmem(), hbm(), vmem()],
-        out_specs=vmem(),
+        out_shape=(jax.ShapeDtypeStruct((rows, channels), BF16), jax.ShapeDtypeStruct((8, TILE), F32)),
+        in_specs=[vmem()] + [hbm()] * 6,
+        out_specs=(vmem(), vmem()),
         scratch_shapes=[
+            VM((2, SIDE, block, channels), BF16),
             VM((2, SIDE, block, channels), BF16),
             VM((2, SIDE, block, channels), BF16),
             VM((2, 2, block // 2, channels), BF16),
@@ -489,16 +488,22 @@
             VM((2, 2, seg // 2, channels), BF16),
             VM((2, 2, seg, channels), BF16),
             VM((2, 3, seg, channels), BF16),
-            VM((3,) + cnt.shape, F32),
-            VM((7,) + cnt.shape, F32),
+            VM(cnt, F32),
+            VM((3,) + cnt, F32),
+            VM((7,) + cnt, F32),
             VM((2, seg, channels), BF16),
-            pltpu.SemaphoreType.DMA((2,)),
+            VM((1, slots), jnp.int32),
+            VM((1, slots), jnp.int32),
+            pltpu.SMEM((1,), jnp.int32),
+            VM(links.shape, jnp.int32),
+            VM(weight.shape, BF16),
+            pltpu.SemaphoreType.DMA((7,)),
             pltpu.SemaphoreType.DMA((PLANE_COPIES,)),
             pltpu.SemaphoreType.DMA((PLANE_COPIES,)),
         ],
-        compiler_params=pltpu.CompilerParams(collective_id=0, has_side_effects=True, vmem_limit_bytes=32 * 2**20),
+        compiler_params=pltpu.CompilerParams(collective_id=0, has_side_effects=True, vmem_limit_bytes=40 * MIB),
         name="plane",
-    )(part, cnt, emb, weight)
+    )(part, bi, bu, count, links, emb, weight)
 
 
 def column(part, hits, items, up_weight, down_weight):
@@ -510,6 +515,7 @@
         in_specs=[vmem(), vmem(), hbm(), hbm(), hbm()],
         out_specs=vmem(),
         scratch_shapes=[
+            VM((DEPTH, share, channels), BF16),
             VM((DEPTH, share, channels), BF16),
             VM((DEPTH, share, channels), BF16),
             VM((4, 2, share // 2, channels), BF16),
@@ -523,16 +529,23 @@
             pltpu.SemaphoreType.DMA((COLUMN_COPIES,)),
             pltpu.SemaphoreType.DMA((COLUMN_COPIES,)),
         ],
-        compiler_params=pltpu.CompilerParams(collective_id=1, has_side_effects=True, vmem_limit_bytes=32 * 2**20),
+        compiler_params=pltpu.CompilerParams(collective_id=1, has_side_effects=True, vmem_limit_bytes=40 * MIB),
         name="column",
     )(part, hits, items, up_weight, down_weight)
 
 
+def pin(*xs):
+    return [pltpu.with_memory_space_constraint(x, pltpu.HBM) for x in xs]
+
+
 def body(item_emb, user_emb, block_item, block_user, block_rows, block_count, user_weight, up_weight, down_weight):
-    bi, bu, count = block_item.reshape(-1), block_user.reshape(-1), block_count.reshape(-1)
+    bi, bu, count = block_item.reshape(1, -1), block_user.reshape(1, -1), block_count.reshape(-1)
     links = block_rows.reshape(-1, TILE)
-    user_part, cnt, hits = hop1(bi, bu, count, links, item_emb, user_emb.shape[0])
-    users = plane(user_part, cnt, user_emb, user_weight)
+    bi, bu, links, item_emb, user_emb, user_weight, up_weight, down_weight = pin(
+        bi, bu, links, item_emb, user_emb, user_weight, up_weight, down_weight
+    )
+    user_part = hop1(bi, bu, count, links, item_emb, user_emb.shape[0])
+    users, hits = plane(user_part, bi, bu, count, links, user_emb, user_weight)
     item_part = hop2(bi, bu, count, links, users, item_emb.shape[0])
     return column(item_part, hits, item_emb, up_weight, down_weight)
 

time: 87.5 us -> 76.2 us (0.87)
  local copies, waits for them, and re-layouts: 7.16 us -> 0.66 us
  Pallas kernels: 78.8 us -> 74.5 us
    unnamed x19 -> x1, local copies, waits for them, and re-layouts: 7.16 us -> 0.66 us
    pallas_call x3, Pallas kernels: 53.2 us -> 49 us  [the longest x1 43.6 us: plane(): pl.pallas_call(plane_kernel, out_shape=(jax.ShapeDtypeStruct((rows, chann...]
where the time goes in v2:
time: 76.2 us; the launch traced here: 75.8 us
  Pallas kernels  74.5 us (98%)
    pallas_call x1, Pallas kernels, plane(): pl.pallas_call(plane_kernel, out_shape=(jax.ShapeDtypeStruct((rows, chann...  43.6 us
    pallas_call x1, Pallas kernels, column(): pl.pallas_call(column_kernel, out_shape=jax.ShapeDtypeStruct((share, chan...  25.5 us
    pallas_call x1, Pallas kernels, hop1(): pl.pallas_call(hop1_kernel, out_shape=jax.ShapeDtypeStruct((user_rows, it...  3 us
    pallas_call x1, Pallas kernels, hop2(): pl.pallas_call(hop2_kernel, out_shape=jax.ShapeDtypeStruct((item_rows, us...  2.33 us

profile of v2, /device:TPU:8, one launch (start us, length us, event | category | flops | bytes accessed | tf_op | source)
XLA Modules:
  0.0 75.8 jit_solution(12320390402823167489)
XLA Ops:
  0.7 3.0 %hop1.1.part = f32[6144,256]{1,0:T(8,128)S(1)} custom-call(s32[1,96]{1,0:T(1,128)} %bitcast.10, s32[1,96]{1,0:T(1,128)} %bitcast.13, s32[1]{0:T(128)} %bitcast.4.count_hbm, s32[96,128]{1,0:T(8,128)} %bitcast.7, bf16[4096,256]{1,0:T(8,128)(2,1)} %items.1), custom_call_target="tpu_custom_call" | custom-call | tf_op jit(solution)/shard_map/hop1/pallas_call | solution.py:446
  3.7 43.6 %plane.1 = (bf16[6144,256]{1,0:T(8,128)(2,1)S(1)}, f32[8,128]{1,0:T(8,128)S(1)}) custom-call(f32[6144,256]{1,0:T(8,128)S(1)} %hop1.1.part, s32[1,96]{1,0:T(1,128)} %bitcast.11, s32[1,96]{1,0:T(1,128)} %bitcast.14, s32[1]{0:T(128)} %bitcast.5.count_hbm, s32[96,128]{1,0:T(8,128)} %bitcast.8, bf16[6144,256]{1,0:T(8,128)(2,1)} %emb.1, bf16[256,256]{1,0:T(8,128)(2,1)} %weight_hbm.1), custom_call_target="tpu_custom_call" | custom-call | tf_op jit(solution)/shard_map/plane/pallas_call | solution.py:476
  47.3 2.3 %hop2.1.part = f32[4096,256]{1,0:T(8,128)S(1)} custom-call(s32[1,96]{1,0:T(1,128)} %bitcast.12, s32[1,96]{1,0:T(1,128)} %bitcast.15, s32[1]{0:T(128)} %bitcast.6.count_hbm, s32[96,128]{1,0:T(8,128)} %bitcast.9, bf16[6144,256]{1,0:T(8,128)(2,1)S(1)} %get-tuple-element.7.users), custom_call_target="tpu_custom_call" | custom-call | tf_op jit(solution)/shard_map/hop2/pallas_call | solution.py:459
  49.6 25.5 %column.1 = bf16[256,256]{1,0:T(8,128)(2,1)S(1)} custom-call(f32[4096,256]{1,0:T(8,128)S(1)} %hop2.1.part, f32[8,128]{1,0:T(8,128)S(1)} %get-tuple-element.8.hits, bf16[4096,256]{1,0:T(8,128)(2,1)} %items.1, bf16[256,1024]{1,0:T(8,128)(2,1)} %up_weight.1, bf16[1024,256]{1,0:T(8,128)(2,1)} %down_weight.1), custom_call_target="tpu_custom_call" | custom-call | tf_op jit(solution)/shard_map/column/pallas_call | solution.py:512
  75.2 0.7 copy.12

commit v3 on v2

--- a/solution.py
+++ b/solution.py
@@ -12,6 +12,7 @@
 F32 = jnp.float32
 BF16 = jnp.bfloat16
 GROUP = 16
+NOWHERE = 2**10
 VM = pltpu.VMEM
 
 
@@ -26,51 +27,90 @@
     return copies
 
 
-def hop_blocks(from_items, bi, bu, count, links, source, acc):
+def swap_kernel(
+    bi_hbm, bu_hbm, count_hbm, links_hbm, items_hbm, meta, links, found, hits, items, bi, bu, count, local_sem, send_sem, recv_sem
+):
+    slots = links_hbm.shape[0]
+    other = {"edge": 1 - lax.axis_index("edge")}
+    own = links.at[pl.ds(0, slots)]
+    copies = fetch(
+        [(bi_hbm, bi), (bu_hbm, bu), (count_hbm, count), (links_hbm, own), (items_hbm, items)], local_sem
+    )
+    enter([other])
+    w = Wires(send_sem, recv_sem)
+    for copy in copies[:3]:
+        copy.wait()
+    slot = lax.broadcasted_iota(jnp.int32, (1, slots), 1)
+    live = slot < count[0]
+    meta[0:1, 0:slots] = bi[...]
+    meta[1:2, 0:slots] = jnp.where(live, bu[...], NOWHERE)
+    copies[3].wait()
+    w.start(own, links.at[pl.ds(slots, slots)], other)
+    lane = lax.broadcasted_iota(jnp.int32, (slots, TILE), 1)
+    found[...] = row_hits(links[pl.ds(0, slots), :], lane, 0, TILE // 4)
+    w.start(meta.at[pl.ds(0, 8)], meta.at[pl.ds(8, 8)], other)
+    found[...] += row_hits(links[pl.ds(0, slots), :], lane, TILE // 4, TILE // 2)
+    slot = lax.broadcasted_iota(jnp.int32, (TILE, slots), 1)
+    tile = lax.broadcasted_iota(jnp.int32, (TILE, slots), 0)
+    chosen = ((tile == bi[...]) & (slot < count[0])).astype(F32).astype(BF16)
+    ones = jnp.ones((8, slots), BF16)
+    hits[...] = lax.dot_general(ones, chosen, (((1,), (1,)), ((), ())), preferred_element_type=F32)
+    copies[4].wait()
+    for copy in w.made:
+        copy.wait_recv()
+    w.finish()
+
+
+def row_hits(links, lane, first, last):
+    found = jnp.zeros(lane.shape, F32)
+    for r in range(first, last):
+        found += (links[:, r : r + 1] == lane).astype(F32)
+    return found
+
+
+def hop_kernel(from_items, half_tiles, meta_ref, links, source, acc, meta, src, dst, slot, sem):
+    e = lax.axis_index("edge")
+    slots = links.shape[0] // 2
+    copy = fetch([(meta_ref, meta)], sem)[0]
+    groups = 16
+    each = 2 * slots // groups
+    rows = acc.shape[0] // groups
+    copy.wait()
+
+    def choose(g, n):
+        acc[rows_at(g * rows, rows, rows), :] = jnp.zeros((rows, acc.shape[1]), F32)
+        which = g // (groups // 2)
+        base = (g - which * (groups // 2)) * each
+        for j in range(each):
+            ut = meta[which * 8 + 1, base + j] - e * half_tiles
+            ends = meta[which * 8, base + j] * TILE, ut * TILE
+            src[n], dst[n] = ends if from_items else ends[::-1]
+            slot[n] = g * each + j
+            n = n + jnp.where((ut >= 0) & (ut < half_tiles), 1, 0)
+        return n
+
+    count = lax.fori_loop(0, groups, choose, 0)
     inside = lax.broadcasted_iota(jnp.int32, (TILE, TILE), 0)
-    live_count = count[0]
 
     def blocks(group, carry):
         made = []
         for k in range(GROUP):
             b = group * GROUP + k
-            live = b < live_count
-            it = jnp.where(live, bi[0, b], 0)
-            ut = jnp.where(live, bu[0, b], 0)
-            row = jnp.where(live, links[pl.ds(b, 1), :], -1)
+            live = b < count
+            row = jnp.where(live, links[pl.ds(jnp.where(live, slot[b], 0), 1), :], -1)
             onehot = (row == inside).astype(F32).astype(BF16)
-            if from_items:
-                rows = source[rows_at(it * TILE, TILE, TILE), :]
-                made.append((ut, jnp.dot(onehot, rows, preferred_element_type=F32)))
-            else:
-                rows = source[rows_at(ut * TILE, TILE, TILE), :]
-                made.append((it, lax.dot_general(onehot, rows, (((0,), (0,)), ((), ())), preferred_element_type=F32)))
-        for tile, contrib in made:
-            acc[rows_at(tile * TILE, TILE, TILE), :] += contrib
+            rows = source[rows_at(jnp.where(live, src[b], 0), TILE, TILE), :]
+            dims = (((1,), (0,)), ((), ())) if from_items else (((0,), (0,)), ((), ()))
+            contrib = lax.dot_general(onehot, rows, dims, preferred_element_type=F32)
+            made.append((jnp.where(live, dst[b], 0), contrib))
+        for at, contrib in made:
+            acc[rows_at(at, TILE, TILE), :] += contrib
         return carry
 
-    lax.fori_loop(0, (live_count + GROUP - 1) // GROUP, blocks, 0)
-
-
-def hop1_kernel(bi_hbm, bu_hbm, count_hbm, links_hbm, items_hbm, acc, bi, bu, count, links, items, sems):
-    copies = fetch(
-        [(items_hbm, items), (links_hbm, links), (bi_hbm, bi), (bu_hbm, bu), (count_hbm, count)], sems
-    )
-    acc[...] = jnp.zeros_like(acc)
-    for copy in copies:
-        copy.wait()
-    hop_blocks(True, bi, bu, count, links, items, acc)
-
-
-def hop2_kernel(bi_hbm, bu_hbm, count_hbm, links_hbm, users, acc, bi, bu, count, links, sems):
-    copies = fetch([(links_hbm, links), (bi_hbm, bi), (bu_hbm, bu), (count_hbm, count)], sems)
-    acc[...] = jnp.zeros_like(acc)
-    for copy in copies:
-        copy.wait()
-    hop_blocks(False, bi, bu, count, links, users, acc)
-
-
-def degrees_of(cnt_ref, hits_ref, found, bi, bu, live_count):
+    lax.fori_loop(0, (count + GROUP - 1) // GROUP, blocks, 0)
+
+
+def degrees_of(cnt_ref, found, bu):
     slots = bu.shape[1]
     triples = cnt_ref.shape[1]
     which = lax.broadcasted_iota(jnp.int32, (triples, slots), 0) * 3
@@ -82,11 +122,6 @@
     cnt_ref[1] = jnp.where(lanes < 32, pltpu.roll(a, 32, 1), pltpu.roll(b, 32, 1))
     cnt_ref[2] = jnp.where(lanes < 64, pltpu.roll(b, 64, 1), pltpu.roll(c, 64, 1))
     cnt_ref[3] = pltpu.roll(c, 96, 1)
-    slot = lax.broadcasted_iota(jnp.int32, (TILE, slots), 1)
-    tile = lax.broadcasted_iota(jnp.int32, (TILE, slots), 0)
-    chosen = ((tile == bi) & (slot < live_count)).astype(F32).astype(BF16)
-    ones = jnp.ones((8, slots), BF16)
-    hits_ref[...] = lax.dot_general(ones, chosen, (((1,), (1,)), ((), ())), preferred_element_type=F32)
 
 
 class Wires:
@@ -124,16 +159,16 @@
 
 
 SIDE = 4
-PLANE_COPIES = 111
+PLANE_COPIES = 69
 
 
 def plane_kernel(
-    part, bi_hbm, bu_hbm, count_hbm, links_hbm, emb, weight_hbm, users, hits, to_core, from_core, sums, opposite, final, total,
-    opposite2, final2, small, cnt, total_cnt, got_cnt, own_rows, bi, bu, count, links, weight, local_sem, send_sem, recv_sem,
+    part, meta, links, found, emb, weight_hbm, users, sums, opposite, final, total, opposite2, final2, small, cnt, total_cnt,
+    got_cnt, own_rows, weight, local_sem, send_sem, recv_sem,
 ):
     item, e = lax.axis_index("item"), lax.axis_index("edge")
     x, y = item // SIDE, item % SIDE
-    seg = part.shape[0] // (2 * 2 * SIDE * SIDE)
+    seg = part.shape[0] // (2 * SIDE * SIDE)
     block = SIDE * seg
     half, half2 = block // 2, seg // 2
 
@@ -150,59 +185,40 @@
     p1, p2 = (x, y), (y, x)
     ring1, ring2 = (along_x, along_y), (along_y, along_x)
 
-    def block_at(core, h, k1):
-        return ((core * 2 + h) * SIDE + step(p1[h], k1)) * block
-
-    def seg_at(core, h, k1, k2):
-        return block_at(core, h, k1) + step(p2[h], k2) * seg
+    def block_at(h, k1):
+        return (h * SIDE + step(p1[h], k1)) * block
+
+    def seg_at(h, k1, k2):
+        return block_at(h, k1) + step(p2[h], k2) * seg
 
     own_copies = fetch(
-        [(emb.at[rows_at(seg_at(e, h, 0, 0), seg, seg)], own_rows.at[h]) for h in range(2)]
-        + [(links_hbm, links), (bi_hbm, bi), (bu_hbm, bu), (count_hbm, count), (weight_hbm, weight)],
+        [(emb.at[rows_at(e * part.shape[0] + seg_at(h, 0, 0), seg, seg)], own_rows.at[h]) for h in range(2)]
+        + [(weight_hbm, weight)],
         local_sem,
     )
-    enter([along_x(1), along_x(-1), along_y(1), along_y(-1), other])
+
+    def mine(h, k, start, size):
+        return part[rows_at(block_at(h, k) + start, size, half2), :]
+
+    for h in range(2):
+        sums[h, 2] = mine(h, 2, 0, block).astype(BF16)
+        sums[h, 1, pl.ds(half, half)] = mine(h, 1, half, half).astype(BF16)
+        sums[h, 3, pl.ds(0, half)] = mine(h, 3, 0, half).astype(BF16)
+    enter([along_x(1), along_x(-1), along_x(2), along_y(1), along_y(-1), along_y(2), other])
     w = Wires(send_sem, recv_sem)
 
-    core_sums = {}
-    for k in (2, 1, 3, 0):
-        for h in range(2):
-            to_core[h, k] = part[rows_at(block_at(1 - e, h, k), block, seg), :].astype(BF16)
-            core_sums[h, k] = w.start(to_core.at[h, k], from_core.at[h, k], other)
-
-    for copy in own_copies[2:6]:
-        copy.wait()
-    slots = links.shape[0]
-    live = lax.broadcasted_iota(jnp.int32, (slots, TILE), 0) < count[0]
-    lane = lax.broadcasted_iota(jnp.int32, (slots, TILE), 1)
-    masked = jnp.where(live, links[...], -1)
-
-    def column_hits(first, last):
-        found = jnp.zeros((slots, TILE), F32)
-        for r in range(first, last):
-            found += (masked[:, r : r + 1] == lane).astype(F32)
-        return found
-
-    found = column_hits(0, TILE // 2)
-
-    def mine(h, k, start, size):
-        return part[rows_at(block_at(e, h, k) + start, size, half2), :] + up(from_core[h, k, pl.ds(start, size), :])
-
-    to_far = {}
-    for h in range(2):
-        core_sums[h, 2].wait_recv()
-        sums[h, 2] = mine(h, 2, 0, block).astype(BF16)
+    to_far, near = {}, {}
+    for h in range(2):
         to_far[h, 1] = w.start(sums.at[h, 2, pl.ds(0, half)], opposite.at[h, 0], ring1[h](1))
         to_far[h, -1] = w.start(sums.at[h, 2, pl.ds(half, half)], opposite.at[h, 1], ring1[h](-1))
-    near = {}
-    for h in range(2):
-        core_sums[h, 1].wait_recv()
-        sums[h, 1, pl.ds(half, half)] = mine(h, 1, half, half).astype(BF16)
+    for h in range(2):
         near[h, 1, 0] = w.start(sums.at[h, 1, pl.ds(half, half)], final.at[h, 0, pl.ds(half, half)], ring1[h](1))
-        core_sums[h, 3].wait_recv()
-        sums[h, 3, pl.ds(0, half)] = mine(h, 3, 0, half).astype(BF16)
         near[h, -1, 0] = w.start(sums.at[h, 3, pl.ds(0, half)], final.at[h, 1, pl.ds(0, half)], ring1[h](-1))
-    degrees_of(cnt, hits, (found + column_hits(TILE // 2, TILE)).astype(BF16), bi[...], bu[...], count[0])
+
+    slots = found.shape[0]
+    lane = lax.broadcasted_iota(jnp.int32, (slots, TILE), 1)
+    hits = found[...] + row_hits(links[pl.ds(0, slots), :], lane, TILE // 2, TILE)
+    degrees_of(cnt, hits.astype(BF16), meta[1:2, 0:slots])
     core_cnt = w.start(cnt, got_cnt.at[0], other)
     for h in range(2):
         to_far[h, 1].wait_recv()
@@ -213,19 +229,12 @@
         near[h, -1, 1] = w.start(sums.at[h, 3, pl.ds(half, half)], final.at[h, 1, pl.ds(half, half)], ring1[h](-1))
     core_cnt.wait_recv()
     total_cnt[0] = cnt[...] + got_cnt[0]
-    cnt_x = [w.start(total_cnt.at[0], got_cnt.at[1], along_x(1)), w.start(total_cnt.at[0], got_cnt.at[2], along_x(-1))]
-    for h in range(2):
-        core_sums[h, 0].wait_recv()
+    cnt_x = [w.start(total_cnt.at[0], got_cnt.at[1 + k], along_x(by)) for k, by in enumerate((1, -1, 2))]
+    for h in range(2):
         near[h, 1, 0].wait_recv()
         near[h, -1, 0].wait_recv()
         total[h, pl.ds(0, half)] = mine(h, 0, 0, half) + up(final[h, 1, pl.ds(0, half)])
         total[h, pl.ds(half, half)] = mine(h, 0, half, half) + up(final[h, 0, pl.ds(half, half)])
-    cnt_x[0].wait_recv()
-    cnt_x.append(w.start(got_cnt.at[1], got_cnt.at[3], along_x(1)))
-    cnt_x[1].wait_recv()
-    cnt_x[2].wait_recv()
-    total_cnt[1] = total_cnt[0] + got_cnt[1] + got_cnt[2] + got_cnt[3]
-    cnt_y = [w.start(total_cnt.at[1], got_cnt.at[4], along_y(1)), w.start(total_cnt.at[1], got_cnt.at[5], along_y(-1))]
 
     def ready(h, k, start, size):
         return total[h, rows_at(step(p2[h], k) * seg + start, size, half2), :]
@@ -243,8 +252,10 @@
         near2[h, 1, 0] = w.start(small.at[h, 1, pl.ds(half2, half2)], final2.at[h, 0, pl.ds(half2, half2)], ring2[h](1))
         small[h, 2, pl.ds(0, half2)] = ready(h, -1, 0, half2).astype(BF16)
         near2[h, -1, 0] = w.start(small.at[h, 2, pl.ds(0, half2)], final2.at[h, 1, pl.ds(0, half2)], ring2[h](-1))
-    cnt_y[0].wait_recv()
-    cnt_y.append(w.start(got_cnt.at[4], got_cnt.at[6], along_y(1)))
+    for copy in cnt_x:
+        copy.wait_recv()
+    total_cnt[1] = total_cnt[0] + got_cnt[1] + got_cnt[2] + got_cnt[3]
+    cnt_y = [w.start(total_cnt.at[1], got_cnt.at[4 + k], along_y(by)) for k, by in enumerate((1, -1, 2))]
     for h in range(2):
         to_far2[h, 1].wait_recv()
         small[h, 1, pl.ds(0, half2)] = (ready(h, 1, 0, half2) + up(opposite2[h, 0])).astype(BF16)
@@ -252,73 +263,65 @@
         to_far2[h, -1].wait_recv()
         small[h, 2, pl.ds(half2, half2)] = (ready(h, -1, half2, half2) + up(opposite2[h, 1])).astype(BF16)
         near2[h, -1, 1] = w.start(small.at[h, 2, pl.ds(half2, half2)], final2.at[h, 1, pl.ds(half2, half2)], ring2[h](-1))
-    cnt_y[1].wait_recv()
-    cnt_y[2].wait_recv()
+    for copy in cnt_y:
+        copy.wait_recv()
     total_cnt[2] = total_cnt[1] + got_cnt[4] + got_cnt[5] + got_cnt[6]
 
-    for h in (0, 1, 6):
-        own_copies[h].wait()
+    for copy in own_copies:
+        copy.wait()
     own_diag = lax.broadcasted_iota(jnp.int32, (seg, TILE), 0) == lax.broadcasted_iota(jnp.int32, (seg, TILE), 1)
+    degrees = []
     for h in range(2):
         degree = total_cnt[2, step(p2[h], 0), pl.ds((e * 2 + h) * SIDE + p1[h], 1), :]
         degree = jnp.sum(jnp.where(own_diag, jnp.broadcast_to(degree, (seg, TILE)), 0.0), axis=1, keepdims=True)
+        degrees.append(jnp.maximum(degree, 1.0))
+    for h in range(2):
         for s in (1, -1):
             near2[h, s, 0].wait_recv()
             near2[h, s, 1].wait_recv()
         summed = ready(h, 0, 0, seg) + up(final2[h, 0]) + up(final2[h, 1])
-        average = (summed / jnp.maximum(degree, 1.0)).astype(BF16)
+        average = (summed / degrees[h]).astype(BF16)
         v = jnp.dot(average, weight[...], preferred_element_type=F32)
         fresh = up(own_rows[h]) + v / (1.0 + jnp.exp(-v))
-        users[rows_at(seg_at(e, h, 0, 0), seg, seg), :] = fresh.astype(BF16)
+        users[rows_at(seg_at(h, 0, 0), seg, seg), :] = fresh.astype(BF16)
 
     def send(h, k1, k2, start, size, device):
-        there = users.at[rows_at(seg_at(e, h, k1, k2) + start, size, half2)]
+        there = users.at[rows_at(seg_at(h, k1, k2) + start, size, half2)]
         return w.start(there, there, device)
 
-    c1, c1f, c2, c2f, d = {}, {}, {}, {}, []
+    c1, c2, c2f = {}, {}, {}
 
     def spread(h, k2):
         for s in (1, -1):
             c2[h, k2, s] = send(h, 0, k2, 0, seg, ring1[h](s))
-        d.append(send(h, 0, k2, 0, seg, other))
 
     def relay(h, k2):
         c2[h, k2, 1].wait_recv()
         c2f[h, k2, 1] = send(h, -1, k2, 0, half2, ring1[h](1))
-        d.append(send(h, -1, k2, 0, seg, other))
         c2[h, k2, -1].wait_recv()
         c2f[h, k2, -1] = send(h, 1, k2, half2, half2, ring1[h](-1))
-        d.append(send(h, 1, k2, 0, seg, other))
-
+
+    for h in range(2):
+        for s in (1, -1, 2):
+            c1[h, s] = send(h, 0, 0, 0, seg, ring2[h](s))
+    for h in range(2):
+        spread(h, 0)
     for h in range(2):
         for s in (1, -1):
-            c1[h, s] = send(h, 0, 0, 0, seg, ring2[h](s))
-        spread(h, 0)
-    for h in range(2):
-        c1[h, 1].wait_recv()
-        c1f[h, 1] = send(h, 0, -1, 0, half2, ring2[h](1))
-        c1[h, -1].wait_recv()
-        c1f[h, -1] = send(h, 0, 1, half2, half2, ring2[h](-1))
-        spread(h, -1)
-        spread(h, 1)
+            c1[h, s].wait_recv()
+            spread(h, -s)
     for h in range(2):
         relay(h, 0)
     for h in range(2):
-        c1f[h, 1].wait_recv()
-        c1f[h, -1].wait_recv()
+        c1[h, 2].wait_recv()
         spread(h, 2)
     for k2 in (-1, 1, 2):
         for h in range(2):
             relay(h, k2)
-    for k2 in (0, -1, 1, 2):
-        for h in range(2):
-            c2f[h, k2, 1].wait_recv()
-            c2f[h, k2, -1].wait_recv()
-            d.append(send(h, 2, k2, 0, seg, other))
-    for copy in d:
+    for copy in c2f.values():
         copy.wait_recv()
     w.finish()
-    assert len(w.made) <= PLANE_COPIES, len(w.made)
+    assert len(w.made) == PLANE_COPIES, len(w.made)
 
 
 DEPTH = 8
@@ -438,49 +441,58 @@
 MIB = 2**20
 
 
-def lists(slots):
-    return [pltpu.SMEM((1, slots), jnp.int32), pltpu.SMEM((1, slots), jnp.int32), pltpu.SMEM((1,), jnp.int32)]
-
-
-def hop1(bi, bu, count, links, items, user_rows):
+def swap(bi, bu, count, links, items):
+    slots = links.shape[0]
     return pl.pallas_call(
-        hop1_kernel,
-        out_shape=jax.ShapeDtypeStruct((user_rows, items.shape[1]), F32),
+        swap_kernel,
+        out_shape=(
+            jax.ShapeDtypeStruct((16, TILE), jnp.int32),
+            jax.ShapeDtypeStruct((2 * slots, TILE), jnp.int32),
+            jax.ShapeDtypeStruct((slots, TILE), F32),
+            jax.ShapeDtypeStruct((8, TILE), F32),
+            jax.ShapeDtypeStruct(items.shape, BF16),
+        ),
         in_specs=[hbm()] * 5,
+        out_specs=(vmem(),) * 5,
+        scratch_shapes=[
+            VM((1, slots), jnp.int32),
+            VM((1, slots), jnp.int32),
+            pltpu.SMEM((1,), jnp.int32),
+            pltpu.SemaphoreType.DMA((5,)),
+            pltpu.SemaphoreType.DMA((2,)),
+            pltpu.SemaphoreType.DMA((2,)),
+        ],
+        compiler_params=pltpu.CompilerParams(collective_id=2, has_side_effects=True, vmem_limit_bytes=16 * MIB),
+        name="swap",
+    )(bi, bu, count, links, items)
+
+
+def hop(from_items, meta, links, source, rows, half_tiles):
+    slots = links.shape[0]
+    return pl.pallas_call(
+        functools.partial(hop_kernel, from_items, half_tiles),
+        out_shape=jax.ShapeDtypeStruct((rows, source.shape[1]), F32),
+        in_specs=[vmem()] * 3,
         out_specs=vmem(),
-        scratch_shapes=lists(bi.shape[1])
-        + [VM(links.shape, jnp.int32), VM(items.shape, BF16), pltpu.SemaphoreType.DMA((5,))],
-        compiler_params=pltpu.CompilerParams(vmem_limit_bytes=40 * MIB),
-        name="hop1",
-    )(bi, bu, count, links, items)
-
-
-def hop2(bi, bu, count, links, users, item_rows):
-    return pl.pallas_call(
-        hop2_kernel,
-        out_shape=jax.ShapeDtypeStruct((item_rows, users.shape[1]), F32),
-        in_specs=[hbm()] * 4 + [vmem()],
-        out_specs=vmem(),
-        scratch_shapes=lists(bi.shape[1]) + [VM(links.shape, jnp.int32), pltpu.SemaphoreType.DMA((4,))],
-        compiler_params=pltpu.CompilerParams(vmem_limit_bytes=40 * MIB),
-        name="hop2",
-    )(bi, bu, count, links, users)
-
-
-def plane(part, bi, bu, count, links, emb, weight):
+        scratch_shapes=[pltpu.SMEM(meta.shape, jnp.int32)]
+        + [pltpu.SMEM((slots + GROUP,), jnp.int32)] * 3
+        + [pltpu.SemaphoreType.DMA((1,))],
+        compiler_params=pltpu.CompilerParams(vmem_limit_bytes=24 * MIB),
+        name="hop1" if from_items else "hop2",
+    )(meta, links, source)
+
+
+def plane(part, meta, links, found, emb, weight):
     rows, channels = part.shape
-    slots = links.shape[0]
-    seg = rows // (4 * SIDE * SIDE)
+    seg = rows // (2 * SIDE * SIDE)
     block = SIDE * seg
-    cnt = (SIDE, rows // (3 * TILE), TILE)
+    cnt = (SIDE, 2 * rows // (3 * TILE), TILE)
     return pl.pallas_call(
         plane_kernel,
-        out_shape=(jax.ShapeDtypeStruct((rows, channels), BF16), jax.ShapeDtypeStruct((8, TILE), F32)),
-        in_specs=[vmem()] + [hbm()] * 6,
-        out_specs=(vmem(), vmem()),
+        out_shape=jax.ShapeDtypeStruct((rows, channels), BF16),
+        in_specs=[vmem()] * 4 + [hbm()] * 2,
+        out_specs=vmem(),
         scratch_shapes=[
-            VM((2, SIDE, block, channels), BF16),
-            VM((2, SIDE, block, channels), BF16),
             VM((2, SIDE, block, channels), BF16),
             VM((2, 2, block // 2, channels), BF16),
             VM((2, 2, block, channels), BF16),
@@ -492,18 +504,14 @@
             VM((3,) + cnt, F32),
             VM((7,) + cnt, F32),
             VM((2, seg, channels), BF16),
-            VM((1, slots), jnp.int32),
-            VM((1, slots), jnp.int32),
-            pltpu.SMEM((1,), jnp.int32),
-            VM(links.shape, jnp.int32),
             VM(weight.shape, BF16),
-            pltpu.SemaphoreType.DMA((7,)),
+            pltpu.SemaphoreType.DMA((3,)),
             pltpu.SemaphoreType.DMA((PLANE_COPIES,)),
             pltpu.SemaphoreType.DMA((PLANE_COPIES,)),
         ],
-        compiler_params=pltpu.CompilerParams(collective_id=0, has_side_effects=True, vmem_limit_bytes=40 * MIB),
+        compiler_params=pltpu.CompilerParams(collective_id=0, has_side_effects=True, vmem_limit_bytes=32 * MIB),
         name="plane",
-    )(part, bi, bu, count, links, emb, weight)
+    )(part, meta, links, found, emb, weight)
 
 
 def column(part, hits, items, up_weight, down_weight):
@@ -544,9 +552,11 @@
     bi, bu, links, item_emb, user_emb, user_weight, up_weight, down_weight = pin(
         bi, bu, links, item_emb, user_emb, user_weight, up_weight, down_weight
     )
-    user_part = hop1(bi, bu, count, links, item_emb, user_emb.shape[0])
-    users, hits = plane(user_part, bi, bu, count, links, user_emb, user_weight)
-    item_part = hop2(bi, bu, count, links, users, item_emb.shape[0])
+    half_rows = user_emb.shape[0] // 2
+    meta, links, found, hits, items = swap(bi, bu, count, links, item_emb)
+    user_part = hop(True, meta, links, items, half_rows, half_rows // TILE)
+    users = plane(user_part, meta, links, found, user_emb, user_weight)
+    item_part = hop(False, meta, links, users, item_emb.shape[0], half_rows // TILE)
     return column(item_part, hits, item_emb, up_weight, down_weight)
 
 

time: 76.2 us -> 71.5 us (0.938)
  Pallas kernels: 74.5 us -> 69.5 us
    pallas_call x1, Pallas kernels: 25.5 us -> 22.7 us  [column(): pl.pallas_call(column_kernel, out_shape=jax.ShapeDtypeStruct((share, chan...]
    pallas_call x3 -> x4, Pallas kernels: 49 us -> 46.7 us  [the longest x1 36.1 us: plane(): pl.pallas_call(plane_kernel, out_shape=jax.ShapeDtypeStruct((rows, channe...]
where the time goes in v3:
time: 71.5 us; the launch traced here: 70.8 us
  Pallas kernels  69.5 us (97%)
    pallas_call x1, Pallas kernels, plane(): pl.pallas_call(plane_kernel, out_shape=jax.ShapeDtypeStruct((rows, channe...  36.1 us
    pallas_call x1, Pallas kernels, column(): pl.pallas_call(column_kernel, out_shape=jax.ShapeDtypeStruct((share, chan...  22.7 us
    pallas_call x2, Pallas kernels, hop(): pl.pallas_call(functools.partial(hop_kernel, from_items, half_tiles), out...  8.27 us
    pallas_call x1, Pallas kernels, swap(): pl.pallas_call(swap_kernel, out_shape=(jax.ShapeDtypeStruct((16, TILE), j...  2.4 us

profile of v3, /device:TPU:8, one launch (start us, length us, event | category | flops | bytes accessed | tf_op | source)
XLA Modules:
  0.0 70.8 jit_solution(2406096798648913281)
XLA Ops:
  0.7 2.4 %swap.1 = (s32[16,128]{1,0:T(8,128)S(1)}, s32[192,128]{1,0:T(8,128)S(1)}, f32[96,128]{1,0:T(8,128)S(1)}, f32[8,128]{1,0:T(8,128)S(1)}, bf16[4096,256]{1,0:T(8,128)(2,1)S(1)}) custom-call(s32[1,96]{1,0:T(1,128)} %bitcast.6, s32[1,96]{1,0:T(1,128)} %bitcast.7, s32[1]{0:T(128)} %bitcast.4.count_hbm, s32[96,128]{1,0:T(8,128)} %bitcast.5, bf16[4096,256]{1,0:T(8,128)(2,1)} %items.1), custom_call_target="tpu_custom_call" | custom-call | tf_op jit(solution)/shard_map/swap/pallas_call | solution.py:446
  3.1 4.0 %hop1.1.part = f32[3072,256]{1,0:T(8,128)S(1)} custom-call(s32[16,128]{1,0:T(8,128)S(1)} %get-tuple-element.10.meta_ref.meta, s32[192,128]{1,0:T(8,128)S(1)} %get-tuple-element.11.links, bf16[4096,256]{1,0:T(8,128)(2,1)S(1)} %get-tuple-element.12.source), custom_call_target="tpu_custom_call" | custom-call | tf_op jit(solution)/shard_map/hop1/pallas_call | solution.py:472
  7.1 36.1 %plane.1.source = bf16[3072,256]{1,0:T(8,128)(2,1)S(1)} custom-call(f32[3072,256]{1,0:T(8,128)S(1)} %hop1.1.part, s32[16,128]{1,0:T(8,128)S(1)} %get-tuple-element.10.meta_ref.meta, s32[192,128]{1,0:T(8,128)S(1)} %get-tuple-element.11.links, f32[96,128]{1,0:T(8,128)S(1)} %get-tuple-element.13.found, bf16[6144,256]{1,0:T(8,128)(2,1)} %emb.1, ...), custom_call_target="tpu_custom_call" | custom-call | tf_op jit(solution)/shard_map/plane/pallas_call | solution.py:490
  43.2 4.3 %hop2.1.part = f32[4096,256]{1,0:T(8,128)S(1)} custom-call(s32[16,128]{1,0:T(8,128)S(1)} %get-tuple-element.10.meta_ref.meta, s32[192,128]{1,0:T(8,128)S(1)} %get-tuple-element.11.links, bf16[3072,256]{1,0:T(8,128)(2,1)S(1)} %plane.1.source), custom_call_target="tpu_custom_call" | custom-call | tf_op jit(solution)/shard_map/hop2/pallas_call | solution.py:472
  47.4 22.7 %column.1 = bf16[256,256]{1,0:T(8,128)(2,1)S(1)} custom-call(f32[4096,256]{1,0:T(8,128)S(1)} %hop2.1.part, f32[8,128]{1,0:T(8,128)S(1)} %get-tuple-element.14.hits, bf16[4096,256]{1,0:T(8,128)(2,1)} %items.1, bf16[256,1024]{1,0:T(8,128)(2,1)} %up_weight.1, bf16[1024,256]{1,0:T(8,128)(2,1)} %down_weight.1), custom_call_target="tpu_custom_call" | custom-call | tf_op jit(solution)/shard_map/column/pallas_call | solution.py:520
  70.1 0.7 copy.12

commit v4 on v3

--- a/solution.py
+++ b/solution.py
@@ -112,16 +112,21 @@
 
 def degrees_of(cnt_ref, found, bu):
     slots = bu.shape[1]
-    triples = cnt_ref.shape[1]
+    triples = cnt_ref.shape[0]
     which = lax.broadcasted_iota(jnp.int32, (triples, slots), 0) * 3
     a, b, c = (
         jnp.dot((which + k == bu).astype(F32).astype(BF16), found, preferred_element_type=F32) for k in range(3)
     )
     lanes = lax.broadcasted_iota(jnp.int32, (triples, TILE), 1)
-    cnt_ref[0] = a
-    cnt_ref[1] = jnp.where(lanes < 32, pltpu.roll(a, 32, 1), pltpu.roll(b, 32, 1))
-    cnt_ref[2] = jnp.where(lanes < 64, pltpu.roll(b, 64, 1), pltpu.roll(c, 64, 1))
-    cnt_ref[3] = pltpu.roll(c, 96, 1)
+    quarters = (
+        a,
+        jnp.where(lanes < 32, pltpu.roll(a, 32, 1), pltpu.roll(b, 32, 1)),
+        jnp.where(lanes < 64, pltpu.roll(b, 64, 1), pltpu.roll(c, 64, 1)),
+        pltpu.roll(c, 96, 1),
+    )
+    for j in range(triples):
+        for q, counts in enumerate(quarters):
+            cnt_ref[j, q : q + 1, :] = counts[j : j + 1, :]
 
 
 class Wires:
@@ -159,18 +164,18 @@
 
 
 SIDE = 4
-PLANE_COPIES = 69
+PLANE_COPIES = 103
 
 
 def plane_kernel(
-    part, meta, links, found, emb, weight_hbm, users, sums, opposite, final, total, opposite2, final2, small, cnt, total_cnt,
-    got_cnt, own_rows, weight, local_sem, send_sem, recv_sem,
+    part, meta, links, found, emb, weight_hbm, users, sums, opposite, final, total, small, final2, cnt, got_core, chip_cnt,
+    got_cnt, ring_cnt, got_cnt2, own_rows, weight, local_sem, send_sem, recv_sem,
 ):
     item, e = lax.axis_index("item"), lax.axis_index("edge")
     x, y = item // SIDE, item % SIDE
     seg = part.shape[0] // (2 * SIDE * SIDE)
     block = SIDE * seg
-    half, half2 = block // 2, seg // 2
+    half2 = seg // 2
 
     def step(value, by):
         return lax.rem(value + (by + SIDE), SIDE)
@@ -197,89 +202,109 @@
         local_sem,
     )
 
-    def mine(h, k, start, size):
-        return part[rows_at(block_at(h, k) + start, size, half2), :]
-
-    for h in range(2):
-        sums[h, 2] = mine(h, 2, 0, block).astype(BF16)
-        sums[h, 1, pl.ds(half, half)] = mine(h, 1, half, half).astype(BF16)
-        sums[h, 3, pl.ds(0, half)] = mine(h, 3, 0, half).astype(BF16)
+    def mine(h, k1, k2, start, size):
+        return part[rows_at(seg_at(h, k1, k2) + start, size, half2), :]
+
+    low, high = pl.ds(0, half2), pl.ds(half2, half2)
+    order = (2, 1, -1, 0)
+    for k2 in order:
+        for h in range(2):
+            sums[h, 2, k2 % SIDE] = mine(h, 2, k2, 0, seg).astype(BF16)
+    cnt[...] = jnp.zeros_like(cnt)
     enter([along_x(1), along_x(-1), along_x(2), along_y(1), along_y(-1), along_y(2), other])
     w = Wires(send_sem, recv_sem)
 
-    to_far, near = {}, {}
-    for h in range(2):
-        to_far[h, 1] = w.start(sums.at[h, 2, pl.ds(0, half)], opposite.at[h, 0], ring1[h](1))
-        to_far[h, -1] = w.start(sums.at[h, 2, pl.ds(half, half)], opposite.at[h, 1], ring1[h](-1))
-    for h in range(2):
-        near[h, 1, 0] = w.start(sums.at[h, 1, pl.ds(half, half)], final.at[h, 0, pl.ds(half, half)], ring1[h](1))
-        near[h, -1, 0] = w.start(sums.at[h, 3, pl.ds(0, half)], final.at[h, 1, pl.ds(0, half)], ring1[h](-1))
+    far, near, passed = {}, {}, {}
+
+    def direct(k2):
+        at = k2 % SIDE
+        for h in range(2):
+            sums[h, 1, at, high] = mine(h, 1, k2, half2, half2).astype(BF16)
+            near[h, k2, 1] = w.start(sums.at[h, 1, at, high], final.at[h, 0, at, high], ring1[h](1))
+            sums[h, 3, at, low] = mine(h, -1, k2, 0, half2).astype(BF16)
+            near[h, k2, -1] = w.start(sums.at[h, 3, at, low], final.at[h, 1, at, low], ring1[h](-1))
+
+    def combine(k2):
+        at = k2 % SIDE
+        for h in range(2):
+            far[h, k2, 1].wait_recv()
+            sums[h, 1, at, low] = (mine(h, 1, k2, 0, half2) + up(opposite[h, 0, at])).astype(BF16)
+            passed[h, k2, 1] = w.start(sums.at[h, 1, at, low], final.at[h, 0, at, low], ring1[h](1))
+            far[h, k2, -1].wait_recv()
+            sums[h, 3, at, high] = (mine(h, -1, k2, half2, half2) + up(opposite[h, 1, at])).astype(BF16)
+            passed[h, k2, -1] = w.start(sums.at[h, 3, at, high], final.at[h, 1, at, high], ring1[h](-1))
+
+    def finished(h, k2):
+        for s in (1, -1):
+            near[h, k2, s].wait_recv()
+            passed[h, k2, s].wait_recv()
+        at = k2 % SIDE
+        return mine(h, 0, k2, 0, seg) + up(final[h, 0, at]) + up(final[h, 1, at])
+
+    for k2 in order:
+        at = k2 % SIDE
+        for h in range(2):
+            far[h, k2, 1] = w.start(sums.at[h, 2, at, low], opposite.at[h, 0, at], ring1[h](1))
+            far[h, k2, -1] = w.start(sums.at[h, 2, at, high], opposite.at[h, 1, at], ring1[h](-1))
+    direct(2)
 
     slots = found.shape[0]
     lane = lax.broadcasted_iota(jnp.int32, (slots, TILE), 1)
     hits = found[...] + row_hits(links[pl.ds(0, slots), :], lane, TILE // 2, TILE)
     degrees_of(cnt, hits.astype(BF16), meta[1:2, 0:slots])
-    core_cnt = w.start(cnt, got_cnt.at[0], other)
-    for h in range(2):
-        to_far[h, 1].wait_recv()
-        sums[h, 1, pl.ds(0, half)] = (mine(h, 1, 0, half) + up(opposite[h, 0])).astype(BF16)
-        near[h, 1, 1] = w.start(sums.at[h, 1, pl.ds(0, half)], final.at[h, 0, pl.ds(0, half)], ring1[h](1))
-        to_far[h, -1].wait_recv()
-        sums[h, 3, pl.ds(half, half)] = (mine(h, 3, half, half) + up(opposite[h, 1])).astype(BF16)
-        near[h, -1, 1] = w.start(sums.at[h, 3, pl.ds(half, half)], final.at[h, 1, pl.ds(half, half)], ring1[h](-1))
+    shared = 2 * SIDE
+    core_cnt = w.start(cnt.at[pl.ds((1 - e) * shared, shared)], got_core, other)
+
+    combine(2)
+    direct(1)
+    direct(-1)
     core_cnt.wait_recv()
-    total_cnt[0] = cnt[...] + got_cnt[0]
-    cnt_x = [w.start(total_cnt.at[0], got_cnt.at[1 + k], along_x(by)) for k, by in enumerate((1, -1, 2))]
-    for h in range(2):
-        near[h, 1, 0].wait_recv()
-        near[h, -1, 0].wait_recv()
-        total[h, pl.ds(0, half)] = mine(h, 0, 0, half) + up(final[h, 1, pl.ds(0, half)])
-        total[h, pl.ds(half, half)] = mine(h, 0, half, half) + up(final[h, 0, pl.ds(half, half)])
-
-    def ready(h, k, start, size):
-        return total[h, rows_at(step(p2[h], k) * seg + start, size, half2), :]
-
-    to_far2, near2 = {}, {}
-    for h in range(2):
-        near[h, 1, 1].wait_recv()
-        near[h, -1, 1].wait_recv()
-        total[h, pl.ds(0, half)] += up(final[h, 0, pl.ds(0, half)])
-        total[h, pl.ds(half, half)] += up(final[h, 1, pl.ds(half, half)])
-        small[h, 0] = ready(h, 2, 0, seg).astype(BF16)
-        to_far2[h, 1] = w.start(small.at[h, 0, pl.ds(0, half2)], opposite2.at[h, 0], ring2[h](1))
-        to_far2[h, -1] = w.start(small.at[h, 0, pl.ds(half2, half2)], opposite2.at[h, 1], ring2[h](-1))
-        small[h, 1, pl.ds(half2, half2)] = ready(h, 1, half2, half2).astype(BF16)
-        near2[h, 1, 0] = w.start(small.at[h, 1, pl.ds(half2, half2)], final2.at[h, 0, pl.ds(half2, half2)], ring2[h](1))
-        small[h, 2, pl.ds(0, half2)] = ready(h, -1, 0, half2).astype(BF16)
-        near2[h, -1, 0] = w.start(small.at[h, 2, pl.ds(0, half2)], final2.at[h, 1, pl.ds(0, half2)], ring2[h](-1))
-    for copy in cnt_x:
+    chip_cnt[...] = cnt[pl.ds(e * shared, shared)] + got_core[...]
+    cnt1 = [
+        w.start(chip_cnt.at[h * SIDE + step(p1[h], by)], got_cnt.at[h, k], ring1[h](by))
+        for h in range(2)
+        for k, by in enumerate((1, -1, 2))
+    ]
+    combine(1)
+    combine(-1)
+    direct(0)
+
+    near2 = []
+    for h in range(2):
+        small[h, 0] = finished(h, 2).astype(BF16)
+        near2.append(w.start(small.at[h, 0], final2.at[h, 0], ring2[h](2)))
+    combine(0)
+    for copy in cnt1:
         copy.wait_recv()
-    total_cnt[1] = total_cnt[0] + got_cnt[1] + got_cnt[2] + got_cnt[3]
-    cnt_y = [w.start(total_cnt.at[1], got_cnt.at[4 + k], along_y(by)) for k, by in enumerate((1, -1, 2))]
-    for h in range(2):
-        to_far2[h, 1].wait_recv()
-        small[h, 1, pl.ds(0, half2)] = (ready(h, 1, 0, half2) + up(opposite2[h, 0])).astype(BF16)
-        near2[h, 1, 1] = w.start(small.at[h, 1, pl.ds(0, half2)], final2.at[h, 0, pl.ds(0, half2)], ring2[h](1))
-        to_far2[h, -1].wait_recv()
-        small[h, 2, pl.ds(half2, half2)] = (ready(h, -1, half2, half2) + up(opposite2[h, 1])).astype(BF16)
-        near2[h, -1, 1] = w.start(small.at[h, 2, pl.ds(half2, half2)], final2.at[h, 1, pl.ds(half2, half2)], ring2[h](-1))
-    for copy in cnt_y:
-        copy.wait_recv()
-    total_cnt[2] = total_cnt[1] + got_cnt[4] + got_cnt[5] + got_cnt[6]
+    for h in range(2):
+        ring_cnt[h] = chip_cnt[h * SIDE + step(p1[h], 0)] + got_cnt[h, 0] + got_cnt[h, 1] + got_cnt[h, 2]
+    cnt2 = [
+        w.start(ring_cnt.at[h], got_cnt2.at[h, k], ring2[h](by)) for h in range(2) for k, by in enumerate((1, -1, 2))
+    ]
+    for h in range(2):
+        small[h, 1] = finished(h, 1).astype(BF16)
+        near2.append(w.start(small.at[h, 1], final2.at[h, 1], ring2[h](1)))
+        small[h, 2] = finished(h, -1).astype(BF16)
+        near2.append(w.start(small.at[h, 2], final2.at[h, 2], ring2[h](-1)))
+    for h in range(2):
+        total[h] = finished(h, 0)
 
     for copy in own_copies:
         copy.wait()
+    for copy in cnt2:
+        copy.wait_recv()
     own_diag = lax.broadcasted_iota(jnp.int32, (seg, TILE), 0) == lax.broadcasted_iota(jnp.int32, (seg, TILE), 1)
     degrees = []
     for h in range(2):
-        degree = total_cnt[2, step(p2[h], 0), pl.ds((e * 2 + h) * SIDE + p1[h], 1), :]
+        counts = ring_cnt[h] + got_cnt2[h, 0] + got_cnt2[h, 1] + got_cnt2[h, 2]
+        own_row = lax.broadcasted_iota(jnp.int32, counts.shape, 0) == p2[h]
+        degree = jnp.sum(jnp.where(own_row, counts, 0.0), axis=0, keepdims=True)
         degree = jnp.sum(jnp.where(own_diag, jnp.broadcast_to(degree, (seg, TILE)), 0.0), axis=1, keepdims=True)
         degrees.append(jnp.maximum(degree, 1.0))
-    for h in range(2):
-        for s in (1, -1):
-            near2[h, s, 0].wait_recv()
-            near2[h, s, 1].wait_recv()
-        summed = ready(h, 0, 0, seg) + up(final2[h, 0]) + up(final2[h, 1])
+    for copy in near2:
+        copy.wait_recv()
+    for h in range(2):
+        summed = total[h] + up(final2[h, 0]) + up(final2[h, 1]) + up(final2[h, 2])
         average = (summed / degrees[h]).astype(BF16)
         v = jnp.dot(average, weight[...], preferred_element_type=F32)
         fresh = up(own_rows[h]) + v / (1.0 + jnp.exp(-v))
@@ -294,6 +319,8 @@
     def spread(h, k2):
         for s in (1, -1):
             c2[h, k2, s] = send(h, 0, k2, 0, seg, ring1[h](s))
+        if k2 == 2:
+            c2f[h, k2, 0] = send(h, 0, k2, 0, seg, ring1[h](2))
 
     def relay(h, k2):
         c2[h, k2, 1].wait_recv()
@@ -311,13 +338,14 @@
             c1[h, s].wait_recv()
             spread(h, -s)
     for h in range(2):
-        relay(h, 0)
-    for h in range(2):
         c1[h, 2].wait_recv()
         spread(h, 2)
-    for k2 in (-1, 1, 2):
+    for k2 in (0, -1, 1):
         for h in range(2):
             relay(h, k2)
+    for h in range(2):
+        for s in (1, -1):
+            c2[h, 2, s].wait_recv()
     for copy in c2f.values():
         copy.wait_recv()
     w.finish()
@@ -325,16 +353,17 @@
 
 
 DEPTH = 8
-COLUMN_COPIES = 8 + 14 + 8
+PARTS = 4
+COLUMN_COPIES = 8 + 7 * PARTS + 8
 
 
 def column_kernel(
-    part, hits, items, up_weight, down_weight, out, to_core, from_core, sums, got_up, got_down, chip_hits, got_hits, own_rows, up_v,
-    down_v, local_sem, send_sem, recv_sem,
+    part, hits, items, up_weight, down_weight, out, to_core, from_core, sums, got_up, got_down, chip_hits, got_hits, own_rows, arrived,
+    up_v, down_v, local_sem, send_sem, recv_sem,
 ):
     u, e = lax.axis_index("user"), lax.axis_index("edge")
     share = out.shape[0]
-    half = share // 2
+    half = share // PARTS
 
     def step(by):
         return lax.rem(u + (by + DEPTH), DEPTH)
@@ -384,15 +413,18 @@
         sums[running] = value.astype(BF16)
         wires[s, k, q] = w.start(sums.at[running], got[s].at[k - 1, q], place[s])
 
-    for k in (4, 3):
-        for s in (1, -1):
-            pass_on(s, k, int((s == 1) == (k == 3)))
+    first = [(s, j if s == 1 else PARTS // 2 + j) for j in range(PARTS // 2) for s in (1, -1)]
+    second = [(s, PARTS // 2 + j if s == 1 else j) for j in range(PARTS // 2) for s in (1, -1)]
+    for s, q in first:
+        pass_on(s, 4, q)
+    for s, q in second:
+        pass_on(s, 3, q)
     core_hits.wait_recv()
     chip_hits[...] = hits[...] + got_hits[0]
     for s in (1, -1):
         hit_wires[s, 1] = w.start(chip_hits, got_hits.at[1 if s == 1 else 5], place[s])
     for k in (3, 2, 1):
-        for s, q in ((1, 0), (-1, 1)):
+        for s, q in first:
             pass_on(s, k, q)
         far = 5 - k
         for s in (1, -1):
@@ -401,7 +433,7 @@
                 base = 1 if s == 1 else 5
                 hit_wires[s, far] = w.start(got_hits.at[base + far - 2], got_hits.at[base + far - 1], place[s])
         if k > 1:
-            for s, q in ((1, 1), (-1, 0)):
+            for s, q in second:
                 pass_on(s, k - 1, q)
     hit_wires[1, 4].wait_recv()
     land(0)
@@ -411,17 +443,20 @@
     lane = lax.broadcasted_iota(jnp.int32, degree.shape, 1)
     for copy in local:
         copy.wait()
-    for q in range(2):
+    tile = lax.div(lax.broadcasted_iota(jnp.int32, (share, 1), 0), TILE)
+    own = [jnp.sum(jnp.where(lane == (u * 2 + e) * 2 + k, degree, 0.0)[0:1, :], axis=1, keepdims=True) for k in range(2)]
+    own_degree = jnp.maximum(jnp.where(tile == 0, own[0], own[1]), 1.0)
+    for q in range(PARTS):
         wires[1, 1, q].wait_recv()
         wires[-1, 1, q].wait_recv()
-    for q in range(2):
-        summed = mine(0, q) + up(got_up[0, q]) + up(got_down[0, q])
-        mine_only = jnp.where(lane == (u * 2 + e) * 2 + q, degree, 0.0)
-        own_degree = jnp.sum(mine_only[0:1, :], axis=1, keepdims=True)
-        merged = up(own_rows[pl.ds(q * half, half), :]) + summed / jnp.maximum(own_degree, 1.0)
-        v = jnp.dot(merged.astype(BF16), up_v[...], preferred_element_type=F32)
-        hidden = (v / (1.0 + jnp.exp(-v))).astype(BF16)
-        out[pl.ds(q * half, half), :] = (merged + jnp.dot(hidden, down_v[...], preferred_element_type=F32)).astype(BF16)
+    summed = part[rows_at(chunk(0, e), share, share), :] + up(from_core[0])
+    for q in range(PARTS):
+        rows = pl.ds(q * half, half)
+        arrived[rows, :] = up(got_up[0, q]) + up(got_down[0, q])
+    merged = up(own_rows[...]) + (summed + arrived[...]) / own_degree
+    v = jnp.dot(merged.astype(BF16), up_v[...], preferred_element_type=F32)
+    hidden = (v / (1.0 + jnp.exp(-v))).astype(BF16)
+    out[...] = (merged + jnp.dot(hidden, down_v[...], preferred_element_type=F32)).astype(BF16)
     w.finish()
     assert len(w.made) <= COLUMN_COPIES, len(w.made)
 
@@ -485,24 +520,25 @@
 def plane(part, meta, links, found, emb, weight):
     rows, channels = part.shape
     seg = rows // (2 * SIDE * SIDE)
-    block = SIDE * seg
-    cnt = (SIDE, 2 * rows // (3 * TILE), TILE)
+    pieces = 4 * SIDE
     return pl.pallas_call(
         plane_kernel,
         out_shape=jax.ShapeDtypeStruct((rows, channels), BF16),
         in_specs=[vmem()] * 4 + [hbm()] * 2,
         out_specs=vmem(),
         scratch_shapes=[
-            VM((2, SIDE, block, channels), BF16),
-            VM((2, 2, block // 2, channels), BF16),
-            VM((2, 2, block, channels), BF16),
-            VM((2, block, channels), F32),
-            VM((2, 2, seg // 2, channels), BF16),
-            VM((2, 2, seg, channels), BF16),
+            VM((2, SIDE, SIDE, seg, channels), BF16),
+            VM((2, 2, SIDE, seg // 2, channels), BF16),
+            VM((2, 2, SIDE, seg, channels), BF16),
+            VM((2, seg, channels), F32),
             VM((2, 3, seg, channels), BF16),
-            VM(cnt, F32),
-            VM((3,) + cnt, F32),
-            VM((7,) + cnt, F32),
+            VM((2, 3, seg, channels), BF16),
+            VM((pieces, 8, TILE), F32),
+            VM((pieces // 2, 8, TILE), F32),
+            VM((pieces // 2, 8, TILE), F32),
+            VM((2, 3, 8, TILE), F32),
+            VM((2, 8, TILE), F32),
+            VM((2, 3, 8, TILE), F32),
             VM((2, seg, channels), BF16),
             VM(weight.shape, BF16),
             pltpu.SemaphoreType.DMA((3,)),
@@ -526,11 +562,12 @@
             VM((DEPTH, share, channels), BF16),
             VM((DEPTH, share, channels), BF16),
             VM((DEPTH, share, channels), BF16),
-            VM((4, 2, share // 2, channels), BF16),
-            VM((4, 2, share // 2, channels), BF16),
+            VM((4, PARTS, share // PARTS, channels), BF16),
+            VM((4, PARTS, share // PARTS, channels), BF16),
             VM(hits.shape, F32),
             VM((DEPTH,) + hits.shape, F32),
             VM((share, channels), BF16),
+            VM((share, channels), F32),
             VM(up_weight.shape, BF16),
             VM(down_weight.shape, BF16),
             pltpu.SemaphoreType.DMA((3,)),

time: 71.5 us -> 68.6 us (0.959)
  Pallas kernels: 69.5 us -> 66.8 us
    pallas_call x1, Pallas kernels: 36.1 us -> 32.7 us  [plane(): pl.pallas_call(plane_kernel, out_shape=jax.ShapeDtypeStruct((rows, channe...]
    pallas_call x1, Pallas kernels: 22.7 us -> 23.5 us  [column(): pl.pallas_call(column_kernel, out_shape=jax.ShapeDtypeStruct((share, chan...]
where the time goes in v4:
time: 68.6 us; the launch traced here: 68.2 us
  Pallas kernels  66.8 us (97%)
  between operations  0.69 us (1%)
    pallas_call x1, Pallas kernels, plane(): pl.pallas_call(plane_kernel, out_shape=jax.ShapeDtypeStruct((rows, channe...  32.7 us
    pallas_call x1, Pallas kernels, column(): pl.pallas_call(column_kernel, out_shape=jax.ShapeDtypeStruct((share, chan...  23.5 us
    pallas_call x2, Pallas kernels, hop(): pl.pallas_call(functools.partial(hop_kernel, from_items, half_tiles), out...  8.26 us
    pallas_call x1, Pallas kernels, swap(): pl.pallas_call(swap_kernel, out_shape=(jax.ShapeDtypeStruct((16, TILE), j...  2.4 us

profile of v4, /device:TPU:8, one launch (start us, length us, event | category | flops | bytes accessed | tf_op | source)
XLA Modules:
  0.0 68.2 jit_solution(4166166310217338970)
XLA Ops:
  0.7 2.4 %swap.1 = (s32[16,128]{1,0:T(8,128)S(1)}, s32[192,128]{1,0:T(8,128)S(1)}, f32[96,128]{1,0:T(8,128)S(1)}, f32[8,128]{1,0:T(8,128)S(1)}, bf16[4096,256]{1,0:T(8,128)(2,1)S(1)}) custom-call(s32[1,96]{1,0:T(1,128)} %bitcast.6, s32[1,96]{1,0:T(1,128)} %bitcast.7, s32[1]{0:T(128)} %bitcast.4.count_hbm, s32[96,128]{1,0:T(8,128)} %bitcast.5, bf16[4096,256]{1,0:T(8,128)(2,1)} %items.1), custom_call_target="tpu_custom_call" | custom-call | tf_op jit(solution)/shard_map/swap/pallas_call | solution.py:481
  3.1 4.0 %hop1.1.part = f32[3072,256]{1,0:T(8,128)S(1)} custom-call(s32[16,128]{1,0:T(8,128)S(1)} %get-tuple-element.10.meta_ref.meta, s32[192,128]{1,0:T(8,128)S(1)} %get-tuple-element.11.links, bf16[4096,256]{1,0:T(8,128)(2,1)S(1)} %get-tuple-element.12.source), custom_call_target="tpu_custom_call" | custom-call | tf_op jit(solution)/shard_map/hop1/pallas_call | solution.py:507
  7.1 32.7 %plane.1.source = bf16[3072,256]{1,0:T(8,128)(2,1)S(1)} custom-call(f32[3072,256]{1,0:T(8,128)S(1)} %hop1.1.part, s32[16,128]{1,0:T(8,128)S(1)} %get-tuple-element.10.meta_ref.meta, s32[192,128]{1,0:T(8,128)S(1)} %get-tuple-element.11.links, f32[96,128]{1,0:T(8,128)S(1)} %get-tuple-element.13.found, bf16[6144,256]{1,0:T(8,128)(2,1)} %emb.1, ...), custom_call_target="tpu_custom_call" | custom-call | tf_op jit(solution)/shard_map/plane/pallas_call | solution.py:524
  39.8 4.3 %hop2.1.part = f32[4096,256]{1,0:T(8,128)S(1)} custom-call(s32[16,128]{1,0:T(8,128)S(1)} %get-tuple-element.10.meta_ref.meta, s32[192,128]{1,0:T(8,128)S(1)} %get-tuple-element.11.links, bf16[3072,256]{1,0:T(8,128)(2,1)S(1)} %plane.1.source), custom_call_target="tpu_custom_call" | custom-call | tf_op jit(solution)/shard_map/hop2/pallas_call | solution.py:507
  44.0 23.5 %column.1 = bf16[256,256]{1,0:T(8,128)(2,1)S(1)} custom-call(f32[4096,256]{1,0:T(8,128)S(1)} %hop2.1.part, f32[8,128]{1,0:T(8,128)S(1)} %get-tuple-element.14.hits, bf16[4096,256]{1,0:T(8,128)(2,1)} %items.1, bf16[256,1024]{1,0:T(8,128)(2,1)} %up_weight.1, bf16[1024,256]{1,0:T(8,128)(2,1)} %down_weight.1), custom_call_target="tpu_custom_call" | custom-call | tf_op jit(solution)/shard_map/column/pallas_call | solution.py:556
  67.5 0.7 copy.12

commit v5 on v4

--- a/solution.py
+++ b/solution.py
@@ -13,6 +13,8 @@
 BF16 = jnp.bfloat16
 GROUP = 16
 NOWHERE = 2**10
+ITEM_TILES = 32
+SLOTS = 256
 VM = pltpu.VMEM
 
 
@@ -28,27 +30,38 @@
 
 
 def swap_kernel(
-    bi_hbm, bu_hbm, count_hbm, links_hbm, items_hbm, meta, links, found, hits, items, bi, bu, count, local_sem, send_sem, recv_sem
+    half_tiles, bi_hbm, bu_hbm, count_hbm, links_hbm, items_hbm, meta, links, found, hits, items, bi, bu, count, to_other,
+    local_sem, send_sem, recv_sem,
 ):
     slots = links_hbm.shape[0]
-    other = {"edge": 1 - lax.axis_index("edge")}
+    e = lax.axis_index("edge")
+    other = {"edge": 1 - e}
     own = links.at[pl.ds(0, slots)]
     copies = fetch(
         [(bi_hbm, bi), (bu_hbm, bu), (count_hbm, count), (links_hbm, own), (items_hbm, items)], local_sem
     )
-    enter([other])
-    w = Wires(send_sem, recv_sem)
+    greet([other])
     for copy in copies[:3]:
         copy.wait()
     slot = lax.broadcasted_iota(jnp.int32, (1, slots), 1)
     live = slot < count[0]
-    meta[0:1, 0:slots] = bi[...]
+
+    def codes(core, first):
+        ut = bu[...] - core * half_tiles
+        code = (ut * ITEM_TILES + bi[...]) * SLOTS + slot + first
+        return jnp.where(live & (ut >= 0) & (ut < half_tiles), code, -1)
+
+    meta[0:1, 0:slots] = codes(e, 0)
     meta[1:2, 0:slots] = jnp.where(live, bu[...], NOWHERE)
+    to_other[...] = jnp.zeros_like(to_other)
+    to_other[0:1, 0:slots] = codes(1 - e, slots)
+    meet([other])
+    w = Wires(send_sem, recv_sem)
     copies[3].wait()
     w.start(own, links.at[pl.ds(slots, slots)], other)
     lane = lax.broadcasted_iota(jnp.int32, (slots, TILE), 1)
     found[...] = row_hits(links[pl.ds(0, slots), :], lane, 0, TILE // 4)
-    w.start(meta.at[pl.ds(0, 8)], meta.at[pl.ds(8, 8)], other)
+    w.start(to_other, meta.at[pl.ds(8, 8)], other)
     found[...] += row_hits(links[pl.ds(0, slots), :], lane, TILE // 4, TILE // 2)
     slot = lax.broadcasted_iota(jnp.int32, (TILE, slots), 1)
     tile = lax.broadcasted_iota(jnp.int32, (TILE, slots), 0)
@@ -68,28 +81,22 @@
     return found
 
 
-def hop_kernel(from_items, half_tiles, meta_ref, links, source, acc, meta, src, dst, slot, sem):
-    e = lax.axis_index("edge")
+def hop_kernel(from_items, meta_ref, links, source, acc, meta, chosen, sem):
     slots = links.shape[0] // 2
     copy = fetch([(meta_ref, meta)], sem)[0]
-    groups = 16
-    each = 2 * slots // groups
-    rows = acc.shape[0] // groups
+    acc[...] = jnp.zeros_like(acc)
     copy.wait()
+    each = 24
 
     def choose(g, n):
-        acc[rows_at(g * rows, rows, rows), :] = jnp.zeros((rows, acc.shape[1]), F32)
-        which = g // (groups // 2)
-        base = (g - which * (groups // 2)) * each
-        for j in range(each):
-            ut = meta[which * 8 + 1, base + j] - e * half_tiles
-            ends = meta[which * 8, base + j] * TILE, ut * TILE
-            src[n], dst[n] = ends if from_items else ends[::-1]
-            slot[n] = g * each + j
-            n = n + jnp.where((ut >= 0) & (ut < half_tiles), 1, 0)
+        for which in range(2):
+            for j in range(each):
+                code = meta[which * 8, g * each + j]
+                chosen[n] = code
+                n = n + 1 + lax.shift_right_arithmetic(code, 31)
         return n
 
-    count = lax.fori_loop(0, groups, choose, 0)
+    count = lax.fori_loop(0, slots // each, choose, 0)
     inside = lax.broadcasted_iota(jnp.int32, (TILE, TILE), 0)
 
     def blocks(group, carry):
@@ -97,12 +104,16 @@
         for k in range(GROUP):
             b = group * GROUP + k
             live = b < count
-            row = jnp.where(live, links[pl.ds(jnp.where(live, slot[b], 0), 1), :], -1)
+            code = jnp.where(live, chosen[b], 0)
+            it = jnp.bitwise_and(lax.shift_right_logical(code, 8), ITEM_TILES - 1) * TILE
+            ut = lax.shift_right_logical(code, 13) * TILE
+            src, dst = (it, ut) if from_items else (ut, it)
+            row = jnp.where(live, links[pl.ds(jnp.bitwise_and(code, SLOTS - 1), 1), :], -1)
             onehot = (row == inside).astype(F32).astype(BF16)
-            rows = source[rows_at(jnp.where(live, src[b], 0), TILE, TILE), :]
+            rows = source[rows_at(src, TILE, TILE), :]
             dims = (((1,), (0,)), ((), ())) if from_items else (((0,), (0,)), ((), ()))
             contrib = lax.dot_general(onehot, rows, dims, preferred_element_type=F32)
-            made.append((jnp.where(live, dst[b], 0), contrib))
+            made.append((dst, contrib))
         for at, contrib in made:
             acc[rows_at(at, TILE, TILE), :] += contrib
         return carry
@@ -152,11 +163,13 @@
             copy.wait_send()
 
 
-def enter(peers):
-    barrier = pltpu.get_barrier_semaphore()
+def greet(peers):
     for peer in peers:
-        pl.semaphore_signal(barrier, inc=1, device_id=peer, device_id_type=MESH)
-    pl.semaphore_wait(barrier, len(peers))
+        pl.semaphore_signal(pltpu.get_barrier_semaphore(), inc=1, device_id=peer, device_id_type=MESH)
+
+
+def meet(peers):
+    pl.semaphore_wait(pltpu.get_barrier_semaphore(), len(peers))
 
 
 def up(x):
@@ -196,6 +209,8 @@
     def seg_at(h, k1, k2):
         return block_at(h, k1) + step(p2[h], k2) * seg
 
+    peers = [along_x(1), along_x(-1), along_x(2), along_y(1), along_y(-1), along_y(2), other]
+    greet(peers)
     own_copies = fetch(
         [(emb.at[rows_at(e * part.shape[0] + seg_at(h, 0, 0), seg, seg)], own_rows.at[h]) for h in range(2)]
         + [(weight_hbm, weight)],
@@ -211,7 +226,7 @@
         for h in range(2):
             sums[h, 2, k2 % SIDE] = mine(h, 2, k2, 0, seg).astype(BF16)
     cnt[...] = jnp.zeros_like(cnt)
-    enter([along_x(1), along_x(-1), along_x(2), along_y(1), along_y(-1), along_y(2), other])
+    meet(peers)
     w = Wires(send_sem, recv_sem)
 
     far, near, passed = {}, {}, {}
@@ -371,6 +386,9 @@
     other = {"edge": 1 - e}
     place = {1: {"user": step(1)}, -1: {"user": step(-1)}}
 
+    peers = [place[1], place[-1], other]
+    greet(peers)
+
     def chunk(k, core):
         return (step(k) * 2 + core) * share
 
@@ -381,13 +399,14 @@
     ]
     for copy in local:
         copy.start()
-    enter([place[1], place[-1], other])
+    for k in (4, 3, -3, 2, -2, 1, -1, 0):
+        to_core[k % DEPTH] = part[rows_at(chunk(k, 1 - e), share, share), :].astype(BF16)
+    meet(peers)
     w = Wires(send_sem, recv_sem)
-    core_hits = w.start(hits, got_hits.at[0], other)
     core = {}
     for k in (4, 3, -3, 2, -2, 1, -1, 0):
-        to_core[k % DEPTH] = part[rows_at(chunk(k, 1 - e), share, share), :].astype(BF16)
         core[k] = w.start(to_core.at[k % DEPTH], from_core.at[k % DEPTH], other)
+    core_hits = w.start(hits, got_hits.at[0], other)
 
     def mine(k, q):
         return part[rows_at(chunk(k, e) + q * half, half, half), :] + up(from_core[k % DEPTH, pl.ds(q * half, half), :])
@@ -476,10 +495,11 @@
 MIB = 2**20
 
 
-def swap(bi, bu, count, links, items):
+def swap(bi, bu, count, links, items, half_tiles):
     slots = links.shape[0]
+    assert items.shape[0] == ITEM_TILES * TILE and 2 * slots <= SLOTS
     return pl.pallas_call(
-        swap_kernel,
+        functools.partial(swap_kernel, half_tiles),
         out_shape=(
             jax.ShapeDtypeStruct((16, TILE), jnp.int32),
             jax.ShapeDtypeStruct((2 * slots, TILE), jnp.int32),
@@ -493,6 +513,7 @@
             VM((1, slots), jnp.int32),
             VM((1, slots), jnp.int32),
             pltpu.SMEM((1,), jnp.int32),
+            VM((8, TILE), jnp.int32),
             pltpu.SemaphoreType.DMA((5,)),
             pltpu.SemaphoreType.DMA((2,)),
             pltpu.SemaphoreType.DMA((2,)),
@@ -502,16 +523,18 @@
     )(bi, bu, count, links, items)
 
 
-def hop(from_items, meta, links, source, rows, half_tiles):
+def hop(from_items, meta, links, source, rows):
     slots = links.shape[0]
     return pl.pallas_call(
-        functools.partial(hop_kernel, from_items, half_tiles),
+        functools.partial(hop_kernel, from_items),
         out_shape=jax.ShapeDtypeStruct((rows, source.shape[1]), F32),
         in_specs=[vmem()] * 3,
         out_specs=vmem(),
-        scratch_shapes=[pltpu.SMEM(meta.shape, jnp.int32)]
-        + [pltpu.SMEM((slots + GROUP,), jnp.int32)] * 3
-        + [pltpu.SemaphoreType.DMA((1,))],
+        scratch_shapes=[
+            pltpu.SMEM(meta.shape, jnp.int32),
+            pltpu.SMEM((slots + GROUP,), jnp.int32),
+            pltpu.SemaphoreType.DMA((1,)),
+        ],
         compiler_params=pltpu.CompilerParams(vmem_limit_bytes=24 * MIB),
         name="hop1" if from_items else "hop2",
     )(meta, links, source)
@@ -590,10 +613,10 @@
         bi, bu, links, item_emb, user_emb, user_weight, up_weight, down_weight
     )
     half_rows = user_emb.shape[0] // 2
-    meta, links, found, hits, items = swap(bi, bu, count, links, item_emb)
-    user_part = hop(True, meta, links, items, half_rows, half_rows // TILE)
+    meta, links, found, hits, items = swap(bi, bu, count, links, item_emb, half_rows // TILE)
+    user_part = hop(True, meta, links, items, half_rows)
     users = plane(user_part, meta, links, found, user_emb, user_weight)
-    item_part = hop(False, meta, links, users, item_emb.shape[0], half_rows // TILE)
+    item_part = hop(False, meta, links, users, item_emb.shape[0])
     return column(item_part, hits, item_emb, up_weight, down_weight)
 
 

time: 68.6 us -> 65.3 us (0.952)
  Pallas kernels: 66.8 us -> 63.4 us
    pallas_call x1, Pallas kernels: 23.5 us -> 21.7 us  [column(): pl.pallas_call(column_kernel, out_shape=jax.ShapeDtypeStruct((share, chan...]
    pallas_call x3, Pallas kernels: 10.7 us -> 9.71 us  [the longest x2 7.31 us: hop(): pl.pallas_call(functools.partial(hop_kernel, from_items), out_shape=jax.S...]
where the time goes in v5:
time: 65.3 us; the launch traced here: 64.8 us
  Pallas kernels  63.4 us (97%)
  between operations  0.69 us (1%)
  local copies, waits for them, and re-layouts  0.66 us (1%)
    pallas_call x1, Pallas kernels, plane(): pl.pallas_call(plane_kernel, out_shape=jax.ShapeDtypeStruct((rows, channe...  32 us
    pallas_call x1, Pallas kernels, column(): pl.pallas_call(column_kernel, out_shape=jax.ShapeDtypeStruct((share, chan...  21.7 us
    pallas_call x2, Pallas kernels, hop(): pl.pallas_call(functools.partial(hop_kernel, from_items), out_shape=jax.S...  7.31 us
    pallas_call x1, Pallas kernels, swap(): pl.pallas_call(functools.partial(swap_kernel, half_tiles), out_shape=(jax...  2.4 us

profile of v5, /device:TPU:8, one launch (start us, length us, event | category | flops | bytes accessed | tf_op | source)
XLA Modules:
  0.0 64.8 jit_solution(10408619088060523690)
XLA Ops:
  0.7 2.4 %swap.1 = (s32[16,128]{1,0:T(8,128)S(1)}, s32[192,128]{1,0:T(8,128)S(1)}, f32[96,128]{1,0:T(8,128)S(1)}, f32[8,128]{1,0:T(8,128)S(1)}, bf16[4096,256]{1,0:T(8,128)(2,1)S(1)}) custom-call(s32[1,96]{1,0:T(1,128)} %bitcast.6, s32[1,96]{1,0:T(1,128)} %bitcast.7, s32[1]{0:T(128)} %bitcast.4.count_hbm, s32[96,128]{1,0:T(8,128)} %bitcast.5, bf16[4096,256]{1,0:T(8,128)(2,1)} %items.1), custom_call_target="tpu_custom_call" | custom-call | tf_op jit(solution)/shard_map/swap/pallas_call | solution.py:501
  3.1 3.5 %hop1.1.part = f32[3072,256]{1,0:T(8,128)S(1)} custom-call(s32[16,128]{1,0:T(8,128)S(1)} %get-tuple-element.10.meta_ref.meta, s32[192,128]{1,0:T(8,128)S(1)} %get-tuple-element.11.links, bf16[4096,256]{1,0:T(8,128)(2,1)S(1)} %get-tuple-element.12.source), custom_call_target="tpu_custom_call" | custom-call | tf_op jit(solution)/shard_map/hop1/pallas_call | solution.py:528
  6.6 32.0 %plane.1.source = bf16[3072,256]{1,0:T(8,128)(2,1)S(1)} custom-call(f32[3072,256]{1,0:T(8,128)S(1)} %hop1.1.part, s32[16,128]{1,0:T(8,128)S(1)} %get-tuple-element.10.meta_ref.meta, s32[192,128]{1,0:T(8,128)S(1)} %get-tuple-element.11.links, f32[96,128]{1,0:T(8,128)S(1)} %get-tuple-element.13.found, bf16[6144,256]{1,0:T(8,128)(2,1)} %emb.1, ...), custom_call_target="tpu_custom_call" | custom-call | tf_op jit(solution)/shard_map/plane/pallas_call | solution.py:547
  38.6 3.8 %hop2.1.part = f32[4096,256]{1,0:T(8,128)S(1)} custom-call(s32[16,128]{1,0:T(8,128)S(1)} %get-tuple-element.10.meta_ref.meta, s32[192,128]{1,0:T(8,128)S(1)} %get-tuple-element.11.links, bf16[3072,256]{1,0:T(8,128)(2,1)S(1)} %plane.1.source), custom_call_target="tpu_custom_call" | custom-call | tf_op jit(solution)/shard_map/hop2/pallas_call | solution.py:528
  42.4 21.7 %column.1 = bf16[256,256]{1,0:T(8,128)(2,1)S(1)} custom-call(f32[4096,256]{1,0:T(8,128)S(1)} %hop2.1.part, f32[8,128]{1,0:T(8,128)S(1)} %get-tuple-element.14.hits, bf16[4096,256]{1,0:T(8,128)(2,1)} %items.1, bf16[256,1024]{1,0:T(8,128)(2,1)} %up_weight.1, bf16[1024,256]{1,0:T(8,128)(2,1)} %down_weight.1), custom_call_target="tpu_custom_call" | custom-call | tf_op jit(solution)/shard_map/column/pallas_call | solution.py:579
  64.1 0.7 %copy.12 = bf16[256,256]{1,0:T(8,128)(2,1)} copy(bf16[256,256]{1,0:T(8,128)(2,1)S(1)} %column.1) | data formatting | bytes 262144

commit v6 on v5

--- a/solution.py
+++ b/solution.py
@@ -11,7 +11,7 @@
 MESH = pl.DeviceIdType.MESH
 F32 = jnp.float32
 BF16 = jnp.bfloat16
-GROUP = 16
+GROUP = 28
 NOWHERE = 2**10
 ITEM_TILES = 32
 SLOTS = 256
@@ -284,10 +284,10 @@
     combine(-1)
     direct(0)
 
-    near2 = []
+    near2 = {0: [], 1: []}
     for h in range(2):
         small[h, 0] = finished(h, 2).astype(BF16)
-        near2.append(w.start(small.at[h, 0], final2.at[h, 0], ring2[h](2)))
+        near2[h].append(w.start(small.at[h, 0], final2.at[h, 0], ring2[h](2)))
     combine(0)
     for copy in cnt1:
         copy.wait_recv()
@@ -298,9 +298,9 @@
     ]
     for h in range(2):
         small[h, 1] = finished(h, 1).astype(BF16)
-        near2.append(w.start(small.at[h, 1], final2.at[h, 1], ring2[h](1)))
+        near2[h].append(w.start(small.at[h, 1], final2.at[h, 1], ring2[h](1)))
         small[h, 2] = finished(h, -1).astype(BF16)
-        near2.append(w.start(small.at[h, 2], final2.at[h, 2], ring2[h](-1)))
+        near2[h].append(w.start(small.at[h, 2], final2.at[h, 2], ring2[h](-1)))
     for h in range(2):
         total[h] = finished(h, 0)
 
@@ -316,37 +316,34 @@
         degree = jnp.sum(jnp.where(own_row, counts, 0.0), axis=0, keepdims=True)
         degree = jnp.sum(jnp.where(own_diag, jnp.broadcast_to(degree, (seg, TILE)), 0.0), axis=1, keepdims=True)
         degrees.append(jnp.maximum(degree, 1.0))
-    for copy in near2:
-        copy.wait_recv()
-    for h in range(2):
+    def send(h, k1, k2, start, size, device):
+        there = users.at[rows_at(seg_at(h, k1, k2) + start, size, half2)]
+        return w.start(there, there, device)
+
+    c1, c2, c2f = {}, {}, {}
+
+    def spread(h, k2):
+        for s in (1, -1):
+            c2[h, k2, s] = send(h, 0, k2, 0, seg, ring1[h](s))
+        if k2 == 2:
+            c2f[h, k2, 0] = send(h, 0, k2, 0, seg, ring1[h](2))
+
+    def relay(h, k2):
+        c2[h, k2, 1].wait_recv()
+        c2f[h, k2, 1] = send(h, -1, k2, 0, half2, ring1[h](1))
+        c2[h, k2, -1].wait_recv()
+        c2f[h, k2, -1] = send(h, 1, k2, half2, half2, ring1[h](-1))
+
+    for h in range(2):
+        for copy in near2[h]:
+            copy.wait_recv()
         summed = total[h] + up(final2[h, 0]) + up(final2[h, 1]) + up(final2[h, 2])
         average = (summed / degrees[h]).astype(BF16)
         v = jnp.dot(average, weight[...], preferred_element_type=F32)
         fresh = up(own_rows[h]) + v / (1.0 + jnp.exp(-v))
         users[rows_at(seg_at(h, 0, 0), seg, seg), :] = fresh.astype(BF16)
-
-    def send(h, k1, k2, start, size, device):
-        there = users.at[rows_at(seg_at(h, k1, k2) + start, size, half2)]
-        return w.start(there, there, device)
-
-    c1, c2, c2f = {}, {}, {}
-
-    def spread(h, k2):
-        for s in (1, -1):
-            c2[h, k2, s] = send(h, 0, k2, 0, seg, ring1[h](s))
-        if k2 == 2:
-            c2f[h, k2, 0] = send(h, 0, k2, 0, seg, ring1[h](2))
-
-    def relay(h, k2):
-        c2[h, k2, 1].wait_recv()
-        c2f[h, k2, 1] = send(h, -1, k2, 0, half2, ring1[h](1))
-        c2[h, k2, -1].wait_recv()
-        c2f[h, k2, -1] = send(h, 1, k2, half2, half2, ring1[h](-1))
-
-    for h in range(2):
         for s in (1, -1, 2):
             c1[h, s] = send(h, 0, 0, 0, seg, ring2[h](s))
-    for h in range(2):
         spread(h, 0)
     for h in range(2):
         for s in (1, -1):
@@ -462,20 +459,24 @@
     lane = lax.broadcasted_iota(jnp.int32, degree.shape, 1)
     for copy in local:
         copy.wait()
-    tile = lax.div(lax.broadcasted_iota(jnp.int32, (share, 1), 0), TILE)
     own = [jnp.sum(jnp.where(lane == (u * 2 + e) * 2 + k, degree, 0.0)[0:1, :], axis=1, keepdims=True) for k in range(2)]
-    own_degree = jnp.maximum(jnp.where(tile == 0, own[0], own[1]), 1.0)
+    own = [jnp.maximum(count, 1.0) for count in own]
     for q in range(PARTS):
-        wires[1, 1, q].wait_recv()
-        wires[-1, 1, q].wait_recv()
-    summed = part[rows_at(chunk(0, e), share, share), :] + up(from_core[0])
-    for q in range(PARTS):
-        rows = pl.ds(q * half, half)
-        arrived[rows, :] = up(got_up[0, q]) + up(got_down[0, q])
-    merged = up(own_rows[...]) + (summed + arrived[...]) / own_degree
-    v = jnp.dot(merged.astype(BF16), up_v[...], preferred_element_type=F32)
-    hidden = (v / (1.0 + jnp.exp(-v))).astype(BF16)
-    out[...] = (merged + jnp.dot(hidden, down_v[...], preferred_element_type=F32)).astype(BF16)
+        arrived[pl.ds(q * half, half), :] = mine(0, q)
+    for pair in ((0, PARTS // 2), (1, PARTS // 2 + 1)):
+        merged = []
+        for q in pair:
+            wires[1, 1, q].wait_recv()
+            wires[-1, 1, q].wait_recv()
+            rows = pl.ds(q * half, half)
+            summed = arrived[rows, :] + up(got_up[0, q]) + up(got_down[0, q])
+            merged.append(up(own_rows[rows, :]) + summed / own[q * half // TILE])
+        merged = jnp.concatenate(merged, axis=0)
+        v = jnp.dot(merged.astype(BF16), up_v[...], preferred_element_type=F32)
+        hidden = (v / (1.0 + jnp.exp(-v))).astype(BF16)
+        fresh = (merged + jnp.dot(hidden, down_v[...], preferred_element_type=F32)).astype(BF16)
+        for at, q in enumerate(pair):
+            out[pl.ds(q * half, half), :] = fresh[at * half : (at + 1) * half]
     w.finish()
     assert len(w.made) <= COLUMN_COPIES, len(w.made)
 

time: 65.3 us -> 65.8 us (level)
    pallas_call x2, Pallas kernels: 7.31 us -> 5.38 us  [hop(): pl.pallas_call(functools.partial(hop_kernel, from_items), out_shape=jax.S...]
    pallas_call x1, Pallas kernels: 21.7 us -> 23.5 us  [column(): pl.pallas_call(column_kernel, out_shape=jax.ShapeDtypeStruct((share, chan...]
where the time goes in v6:
time: 65.8 us; the launch traced here: 64.8 us
  Pallas kernels  63.5 us (97%)
  between operations  0.69 us (1%)
  local copies, waits for them, and re-layouts  0.66 us (1%)
    pallas_call x1, Pallas kernels, plane(): pl.pallas_call(plane_kernel, out_shape=jax.ShapeDtypeStruct((rows, channe...  32.2 us
    pallas_call x1, Pallas kernels, column(): pl.pallas_call(column_kernel, out_shape=jax.ShapeDtypeStruct((share, chan...  23.5 us
    pallas_call x2, Pallas kernels, hop(): pl.pallas_call(functools.partial(hop_kernel, from_items), out_shape=jax.S...  5.38 us
    pallas_call x1, Pallas kernels, swap(): pl.pallas_call(functools.partial(swap_kernel, half_tiles), out_shape=(jax...  2.4 us

profile of v6, /device:TPU:8, one launch (start us, length us, event | category | flops | bytes accessed | tf_op | source)
XLA Modules:
  0.0 64.8 jit_solution(1987119399715424037)
XLA Ops:
  0.7 2.4 %swap.1 = (s32[16,128]{1,0:T(8,128)S(1)}, s32[192,128]{1,0:T(8,128)S(1)}, f32[96,128]{1,0:T(8,128)S(1)}, f32[8,128]{1,0:T(8,128)S(1)}, bf16[4096,256]{1,0:T(8,128)(2,1)S(1)}) custom-call(s32[1,96]{1,0:T(1,128)} %bitcast.6, s32[1,96]{1,0:T(1,128)} %bitcast.7, s32[1]{0:T(128)} %bitcast.4.count_hbm, s32[96,128]{1,0:T(8,128)} %bitcast.5, bf16[4096,256]{1,0:T(8,128)(2,1)} %items.1), custom_call_target="tpu_custom_call" | custom-call | tf_op jit(solution)/shard_map/swap/pallas_call | solution.py:502
  3.1 2.6 %hop1.1.part = f32[3072,256]{1,0:T(8,128)S(1)} custom-call(s32[16,128]{1,0:T(8,128)S(1)} %get-tuple-element.10.meta_ref.meta, s32[192,128]{1,0:T(8,128)S(1)} %get-tuple-element.11.links, bf16[4096,256]{1,0:T(8,128)(2,1)S(1)} %get-tuple-element.12.source), custom_call_target="tpu_custom_call" | custom-call | tf_op jit(solution)/shard_map/hop1/pallas_call | solution.py:529
  5.7 32.2 %plane.1.source = bf16[3072,256]{1,0:T(8,128)(2,1)S(1)} custom-call(f32[3072,256]{1,0:T(8,128)S(1)} %hop1.1.part, s32[16,128]{1,0:T(8,128)S(1)} %get-tuple-element.10.meta_ref.meta, s32[192,128]{1,0:T(8,128)S(1)} %get-tuple-element.11.links, f32[96,128]{1,0:T(8,128)S(1)} %get-tuple-element.13.found, bf16[6144,256]{1,0:T(8,128)(2,1)} %emb.1, ...), custom_call_target="tpu_custom_call" | custom-call | tf_op jit(solution)/shard_map/plane/pallas_call | solution.py:548
  37.9 2.7 %hop2.1.part = f32[4096,256]{1,0:T(8,128)S(1)} custom-call(s32[16,128]{1,0:T(8,128)S(1)} %get-tuple-element.10.meta_ref.meta, s32[192,128]{1,0:T(8,128)S(1)} %get-tuple-element.11.links, bf16[3072,256]{1,0:T(8,128)(2,1)S(1)} %plane.1.source), custom_call_target="tpu_custom_call" | custom-call | tf_op jit(solution)/shard_map/hop2/pallas_call | solution.py:529
  40.6 23.5 %column.1 = bf16[256,256]{1,0:T(8,128)(2,1)S(1)} custom-call(f32[4096,256]{1,0:T(8,128)S(1)} %hop2.1.part, f32[8,128]{1,0:T(8,128)S(1)} %get-tuple-element.14.hits, bf16[4096,256]{1,0:T(8,128)(2,1)} %items.1, bf16[256,1024]{1,0:T(8,128)(2,1)} %up_weight.1, bf16[1024,256]{1,0:T(8,128)(2,1)} %down_weight.1), custom_call_target="tpu_custom_call" | custom-call | tf_op jit(solution)/shard_map/column/pallas_call | solution.py:580
  64.2 0.7 %copy.12 = bf16[256,256]{1,0:T(8,128)(2,1)} copy(bf16[256,256]{1,0:T(8,128)(2,1)S(1)} %column.1) | data formatting | bytes 262144

commit v7 on v6

--- a/solution.py
+++ b/solution.py
@@ -222,10 +222,8 @@
 
     low, high = pl.ds(0, half2), pl.ds(half2, half2)
     order = (2, 1, -1, 0)
-    for k2 in order:
-        for h in range(2):
-            sums[h, 2, k2 % SIDE] = mine(h, 2, k2, 0, seg).astype(BF16)
-    cnt[...] = jnp.zeros_like(cnt)
+    for h in range(2):
+        sums[h, 2, 2] = mine(h, 2, 2, 0, seg).astype(BF16)
     meet(peers)
     w = Wires(send_sem, recv_sem)
 
@@ -259,10 +257,13 @@
     for k2 in order:
         at = k2 % SIDE
         for h in range(2):
+            if k2 != 2:
+                sums[h, 2, at] = mine(h, 2, k2, 0, seg).astype(BF16)
             far[h, k2, 1] = w.start(sums.at[h, 2, at, low], opposite.at[h, 0, at], ring1[h](1))
             far[h, k2, -1] = w.start(sums.at[h, 2, at, high], opposite.at[h, 1, at], ring1[h](-1))
     direct(2)
 
+    cnt[...] = jnp.zeros_like(cnt)
     slots = found.shape[0]
     lane = lax.broadcasted_iota(jnp.int32, (slots, TILE), 1)
     hits = found[...] + row_hits(links[pl.ds(0, slots), :], lane, TILE // 2, TILE)
@@ -396,12 +397,16 @@
     ]
     for copy in local:
         copy.start()
-    for k in (4, 3, -3, 2, -2, 1, -1, 0):
+    def round_off(k):
         to_core[k % DEPTH] = part[rows_at(chunk(k, 1 - e), share, share), :].astype(BF16)
+
+    round_off(4)
     meet(peers)
     w = Wires(send_sem, recv_sem)
     core = {}
     for k in (4, 3, -3, 2, -2, 1, -1, 0):
+        if k != 4:
+            round_off(k)
         core[k] = w.start(to_core.at[k % DEPTH], from_core.at[k % DEPTH], other)
     core_hits = w.start(hits, got_hits.at[0], other)
 

time: 65.8 us -> 66.3 us (level)
  Pallas kernels: 63.5 us -> 64.4 us
    pallas_call x2, Pallas kernels: 5.38 us -> 6.76 us  [hop(): pl.pallas_call(functools.partial(hop_kernel, from_items), out_shape=jax.S...]
where the time goes in v7:
time: 66.3 us; the launch traced here: 65.8 us
  Pallas kernels  64.4 us (97%)
  between operations  0.69 us (1%)
    pallas_call x1, Pallas kernels, plane(): pl.pallas_call(plane_kernel, out_shape=jax.ShapeDtypeStruct((rows, channe...  32.3 us
    pallas_call x1, Pallas kernels, column(): pl.pallas_call(column_kernel, out_shape=jax.ShapeDtypeStruct((share, chan...  22.9 us
    pallas_call x2, Pallas kernels, hop(): pl.pallas_call(functools.partial(hop_kernel, from_items), out_shape=jax.S...  6.76 us
    pallas_call x1, Pallas kernels, swap(): pl.pallas_call(functools.partial(swap_kernel, half_tiles), out_shape=(jax...  2.4 us

profile of v7, /device:TPU:8, one launch (start us, length us, event | category | flops | bytes accessed | tf_op | source)
XLA Modules:
  0.0 65.8 jit_solution(16760753353062179972)
XLA Ops:
  0.7 2.4 %swap.1 = (s32[16,128]{1,0:T(8,128)S(1)}, s32[192,128]{1,0:T(8,128)S(1)}, f32[96,128]{1,0:T(8,128)S(1)}, f32[8,128]{1,0:T(8,128)S(1)}, bf16[4096,256]{1,0:T(8,128)(2,1)S(1)}) custom-call(s32[1,96]{1,0:T(1,128)} %bitcast.6, s32[1,96]{1,0:T(1,128)} %bitcast.7, s32[1]{0:T(128)} %bitcast.4.count_hbm, s32[96,128]{1,0:T(8,128)} %bitcast.5, bf16[4096,256]{1,0:T(8,128)(2,1)} %items.1), custom_call_target="tpu_custom_call" | custom-call | tf_op jit(solution)/shard_map/swap/pallas_call | solution.py:507
  3.1 3.3 %hop1.1.part = f32[3072,256]{1,0:T(8,128)S(1)} custom-call(s32[16,128]{1,0:T(8,128)S(1)} %get-tuple-element.10.meta_ref.meta, s32[192,128]{1,0:T(8,128)S(1)} %get-tuple-element.11.links, bf16[4096,256]{1,0:T(8,128)(2,1)S(1)} %get-tuple-element.12.source), custom_call_target="tpu_custom_call" | custom-call | tf_op jit(solution)/shard_map/hop1/pallas_call | solution.py:534
  6.4 32.3 %plane.1.source = bf16[3072,256]{1,0:T(8,128)(2,1)S(1)} custom-call(f32[3072,256]{1,0:T(8,128)S(1)} %hop1.1.part, s32[16,128]{1,0:T(8,128)S(1)} %get-tuple-element.10.meta_ref.meta, s32[192,128]{1,0:T(8,128)S(1)} %get-tuple-element.11.links, f32[96,128]{1,0:T(8,128)S(1)} %get-tuple-element.13.found, bf16[6144,256]{1,0:T(8,128)(2,1)} %emb.1, ...), custom_call_target="tpu_custom_call" | custom-call | tf_op jit(solution)/shard_map/plane/pallas_call | solution.py:553
  38.7 3.5 %hop2.1.part = f32[4096,256]{1,0:T(8,128)S(1)} custom-call(s32[16,128]{1,0:T(8,128)S(1)} %get-tuple-element.10.meta_ref.meta, s32[192,128]{1,0:T(8,128)S(1)} %get-tuple-element.11.links, bf16[3072,256]{1,0:T(8,128)(2,1)S(1)} %plane.1.source), custom_call_target="tpu_custom_call" | custom-call | tf_op jit(solution)/shard_map/hop2/pallas_call | solution.py:534
  42.1 22.9 %column.1 = bf16[256,256]{1,0:T(8,128)(2,1)S(1)} custom-call(f32[4096,256]{1,0:T(8,128)S(1)} %hop2.1.part, f32[8,128]{1,0:T(8,128)S(1)} %get-tuple-element.14.hits, bf16[4096,256]{1,0:T(8,128)(2,1)} %items.1, bf16[256,1024]{1,0:T(8,128)(2,1)} %up_weight.1, bf16[1024,256]{1,0:T(8,128)(2,1)} %down_weight.1), custom_call_target="tpu_custom_call" | custom-call | tf_op jit(solution)/shard_map/column/pallas_call | solution.py:585
  65.1 0.7 %copy.12 = bf16[256,256]{1,0:T(8,128)(2,1)} copy(bf16[256,256]{1,0:T(8,128)(2,1)S(1)} %column.1) | data formatting | bytes 262144

commit v8 on v7

--- a/solution.py
+++ b/solution.py
@@ -55,14 +55,13 @@
     meta[1:2, 0:slots] = jnp.where(live, bu[...], NOWHERE)
     to_other[...] = jnp.zeros_like(to_other)
     to_other[0:1, 0:slots] = codes(1 - e, slots)
+    copies[3].wait()
     meet([other])
     w = Wires(send_sem, recv_sem)
-    copies[3].wait()
     w.start(own, links.at[pl.ds(slots, slots)], other)
+    w.start(to_other, meta.at[pl.ds(8, 8)], other)
     lane = lax.broadcasted_iota(jnp.int32, (slots, TILE), 1)
     found[...] = row_hits(links[pl.ds(0, slots), :], lane, 0, TILE // 4)
-    w.start(to_other, meta.at[pl.ds(8, 8)], other)
-    found[...] += row_hits(links[pl.ds(0, slots), :], lane, TILE // 4, TILE // 2)
     slot = lax.broadcasted_iota(jnp.int32, (TILE, slots), 1)
     tile = lax.broadcasted_iota(jnp.int32, (TILE, slots), 0)
     chosen = ((tile == bi[...]) & (slot < count[0])).astype(F32).astype(BF16)
@@ -266,7 +265,7 @@
     cnt[...] = jnp.zeros_like(cnt)
     slots = found.shape[0]
     lane = lax.broadcasted_iota(jnp.int32, (slots, TILE), 1)
-    hits = found[...] + row_hits(links[pl.ds(0, slots), :], lane, TILE // 2, TILE)
+    hits = found[...] + row_hits(links[pl.ds(0, slots), :], lane, TILE // 4, TILE)
     degrees_of(cnt, hits.astype(BF16), meta[1:2, 0:slots])
     shared = 2 * SIDE
     core_cnt = w.start(cnt.at[pl.ds((1 - e) * shared, shared)], got_core, other)

time: 66.3 us -> 65.4 us (0.986)
  Pallas kernels: 64.4 us -> 62.8 us
    pallas_call x2, Pallas kernels: 6.76 us -> 5.39 us  [hop(): pl.pallas_call(functools.partial(hop_kernel, from_items), out_shape=jax.S...]
    pallas_call x1, Pallas kernels: 32.3 us -> 33.2 us  [plane(): pl.pallas_call(plane_kernel, out_shape=jax.ShapeDtypeStruct((rows, channe...]
where the time goes in v8:
time: 65.4 us; the launch traced here: 64.2 us
  Pallas kernels  62.8 us (96%)
  between operations  0.69 us (1%)
  local copies, waits for them, and re-layouts  0.66 us (1%)
    pallas_call x1, Pallas kernels, plane(): pl.pallas_call(plane_kernel, out_shape=jax.ShapeDtypeStruct((rows, channe...  33.2 us
    pallas_call x1, Pallas kernels, column(): pl.pallas_call(column_kernel, out_shape=jax.ShapeDtypeStruct((share, chan...  22.3 us
    pallas_call x2, Pallas kernels, hop(): pl.pallas_call(functools.partial(hop_kernel, from_items), out_shape=jax.S...  5.39 us
    pallas_call x1, Pallas kernels, swap(): pl.pallas_call(functools.partial(swap_kernel, half_tiles), out_shape=(jax...  1.94 us

profile of v8, /device:TPU:8, one launch (start us, length us, event | category | flops | bytes accessed | tf_op | source)
XLA Modules:
  0.0 64.2 jit_solution(3807642738465390293)
XLA Ops:
  0.7 1.9 %swap.1 = (s32[16,128]{1,0:T(8,128)S(1)}, s32[192,128]{1,0:T(8,128)S(1)}, f32[96,128]{1,0:T(8,128)S(1)}, f32[8,128]{1,0:T(8,128)S(1)}, bf16[4096,256]{1,0:T(8,128)(2,1)S(1)}) custom-call(s32[1,96]{1,0:T(1,128)} %bitcast.6, s32[1,96]{1,0:T(1,128)} %bitcast.7, s32[1]{0:T(128)} %bitcast.4.count_hbm, s32[96,128]{1,0:T(8,128)} %bitcast.5, bf16[4096,256]{1,0:T(8,128)(2,1)} %items.1), custom_call_target="tpu_custom_call" | custom-call | tf_op jit(solution)/shard_map/swap/pallas_call | solution.py:506
  2.6 2.6 %hop1.1.part = f32[3072,256]{1,0:T(8,128)S(1)} custom-call(s32[16,128]{1,0:T(8,128)S(1)} %get-tuple-element.10.meta_ref.meta, s32[192,128]{1,0:T(8,128)S(1)} %get-tuple-element.11.links, bf16[4096,256]{1,0:T(8,128)(2,1)S(1)} %get-tuple-element.12.source), custom_call_target="tpu_custom_call" | custom-call | tf_op jit(solution)/shard_map/hop1/pallas_call | solution.py:533
  5.2 33.2 %plane.1.source = bf16[3072,256]{1,0:T(8,128)(2,1)S(1)} custom-call(f32[3072,256]{1,0:T(8,128)S(1)} %hop1.1.part, s32[16,128]{1,0:T(8,128)S(1)} %get-tuple-element.10.meta_ref.meta, s32[192,128]{1,0:T(8,128)S(1)} %get-tuple-element.11.links, f32[96,128]{1,0:T(8,128)S(1)} %get-tuple-element.13.found, bf16[6144,256]{1,0:T(8,128)(2,1)} %emb.1, ...), custom_call_target="tpu_custom_call" | custom-call | tf_op jit(solution)/shard_map/plane/pallas_call | solution.py:552
  38.4 2.7 %hop2.1.part = f32[4096,256]{1,0:T(8,128)S(1)} custom-call(s32[16,128]{1,0:T(8,128)S(1)} %get-tuple-element.10.meta_ref.meta, s32[192,128]{1,0:T(8,128)S(1)} %get-tuple-element.11.links, bf16[3072,256]{1,0:T(8,128)(2,1)S(1)} %plane.1.source), custom_call_target="tpu_custom_call" | custom-call | tf_op jit(solution)/shard_map/hop2/pallas_call | solution.py:533
  41.2 22.3 %column.1 = bf16[256,256]{1,0:T(8,128)(2,1)S(1)} custom-call(f32[4096,256]{1,0:T(8,128)S(1)} %hop2.1.part, f32[8,128]{1,0:T(8,128)S(1)} %get-tuple-element.14.hits, bf16[4096,256]{1,0:T(8,128)(2,1)} %items.1, bf16[256,1024]{1,0:T(8,128)(2,1)} %up_weight.1, bf16[1024,256]{1,0:T(8,128)(2,1)} %down_weight.1), custom_call_target="tpu_custom_call" | custom-call | tf_op jit(solution)/shard_map/column/pallas_call | solution.py:584
  63.5 0.7 %copy.12 = bf16[256,256]{1,0:T(8,128)(2,1)} copy(bf16[256,256]{1,0:T(8,128)(2,1)S(1)} %column.1) | data formatting | bytes 262144

commit v9 on v8

--- a/solution.py
+++ b/solution.py
@@ -273,6 +273,8 @@
     combine(2)
     direct(1)
     direct(-1)
+    combine(1)
+    combine(-1)
     core_cnt.wait_recv()
     chip_cnt[...] = cnt[pl.ds(e * shared, shared)] + got_core[...]
     cnt1 = [
@@ -280,8 +282,6 @@
         for h in range(2)
         for k, by in enumerate((1, -1, 2))
     ]
-    combine(1)
-    combine(-1)
     direct(0)
 
     near2 = {0: [], 1: []}

time: 65.4 us -> 66.1 us (1.011); the launches traced: 64.2 us -> 65.8 us
  Pallas kernels: 62.8 us -> 64.4 us
    pallas_call x2, Pallas kernels: 5.39 us -> 6.77 us  [hop(): pl.pallas_call(functools.partial(hop_kernel, from_items), out_shape=jax.S...]
where the time goes in v9:
time: 66.1 us; the launch traced here: 65.8 us
  Pallas kernels  64.4 us (97%)
  between operations  0.69 us (1%)
    pallas_call x1, Pallas kernels, plane(): pl.pallas_call(plane_kernel, out_shape=jax.ShapeDtypeStruct((rows, channe...  33 us
    pallas_call x1, Pallas kernels, column(): pl.pallas_call(column_kernel, out_shape=jax.ShapeDtypeStruct((share, chan...  22.7 us
    pallas_call x2, Pallas kernels, hop(): pl.pallas_call(functools.partial(hop_kernel, from_items), out_shape=jax.S...  6.77 us
    pallas_call x1, Pallas kernels, swap(): pl.pallas_call(functools.partial(swap_kernel, half_tiles), out_shape=(jax...  1.94 us

profile of v9, /device:TPU:8, one launch (start us, length us, event | category | flops | bytes accessed | tf_op | source)
XLA Modules:
  0.0 65.8 jit_solution(145245708866242594)
XLA Ops:
  0.7 1.9 %swap.1 = (s32[16,128]{1,0:T(8,128)S(1)}, s32[192,128]{1,0:T(8,128)S(1)}, f32[96,128]{1,0:T(8,128)S(1)}, f32[8,128]{1,0:T(8,128)S(1)}, bf16[4096,256]{1,0:T(8,128)(2,1)S(1)}) custom-call(s32[1,96]{1,0:T(1,128)} %bitcast.6, s32[1,96]{1,0:T(1,128)} %bitcast.7, s32[1]{0:T(128)} %bitcast.4.count_hbm, s32[96,128]{1,0:T(8,128)} %bitcast.5, bf16[4096,256]{1,0:T(8,128)(2,1)} %items.1), custom_call_target="tpu_custom_call" | custom-call | tf_op jit(solution)/shard_map/swap/pallas_call | solution.py:506
  2.6 3.3 %hop1.1.part = f32[3072,256]{1,0:T(8,128)S(1)} custom-call(s32[16,128]{1,0:T(8,128)S(1)} %get-tuple-element.10.meta_ref.meta, s32[192,128]{1,0:T(8,128)S(1)} %get-tuple-element.11.links, bf16[4096,256]{1,0:T(8,128)(2,1)S(1)} %get-tuple-element.12.source), custom_call_target="tpu_custom_call" | custom-call | tf_op jit(solution)/shard_map/hop1/pallas_call | solution.py:533
  5.9 33.0 %plane.1.source = bf16[3072,256]{1,0:T(8,128)(2,1)S(1)} custom-call(f32[3072,256]{1,0:T(8,128)S(1)} %hop1.1.part, s32[16,128]{1,0:T(8,128)S(1)} %get-tuple-element.10.meta_ref.meta, s32[192,128]{1,0:T(8,128)S(1)} %get-tuple-element.11.links, f32[96,128]{1,0:T(8,128)S(1)} %get-tuple-element.13.found, bf16[6144,256]{1,0:T(8,128)(2,1)} %emb.1, ...), custom_call_target="tpu_custom_call" | custom-call | tf_op jit(solution)/shard_map/plane/pallas_call | solution.py:552
  38.9 3.5 %hop2.1.part = f32[4096,256]{1,0:T(8,128)S(1)} custom-call(s32[16,128]{1,0:T(8,128)S(1)} %get-tuple-element.10.meta_ref.meta, s32[192,128]{1,0:T(8,128)S(1)} %get-tuple-element.11.links, bf16[3072,256]{1,0:T(8,128)(2,1)S(1)} %plane.1.source), custom_call_target="tpu_custom_call" | custom-call | tf_op jit(solution)/shard_map/hop2/pallas_call | solution.py:533
  42.4 22.7 %column.1 = bf16[256,256]{1,0:T(8,128)(2,1)S(1)} custom-call(f32[4096,256]{1,0:T(8,128)S(1)} %hop2.1.part, f32[8,128]{1,0:T(8,128)S(1)} %get-tuple-element.14.hits, bf16[4096,256]{1,0:T(8,128)(2,1)} %items.1, bf16[256,1024]{1,0:T(8,128)(2,1)} %up_weight.1, bf16[1024,256]{1,0:T(8,128)(2,1)} %down_weight.1), custom_call_target="tpu_custom_call" | custom-call | tf_op jit(solution)/shard_map/column/pallas_call | solution.py:584
  65.1 0.7 %copy.12 = bf16[256,256]{1,0:T(8,128)(2,1)} copy(bf16[256,256]{1,0:T(8,128)(2,1)S(1)} %column.1) | data formatting | bytes 262144
